TPU v7x, 16 devices: a whole 2x2x2 slice. The times are simulated.
16 devices in a mesh: tp: 4 (over z, y), dp: 4 (over x, core).
Axes of the slice: x: 2, y: 2, z: 2, core: 2. Of those that a mesh axis runs over, the one named last changes fastest.
Arguments:
- x_in: bfloat16 [2, 128, 4096], P(None, ('dp', 'tp'))
- w_gate: bfloat16 [4096, 14336], P('dp', 'tp')
- w_up: bfloat16 [4096, 14336], P('dp', 'tp')
- w_down: bfloat16 [14336, 4096], P('tp', 'dp')
- grad_y: bfloat16 [2, 128, 4096], P(None, ('dp', 'tp'))
Outputs:
- output 1: bfloat16 [2, 128, 4096], P(None, ('dp', 'tp'))
- output 2: bfloat16 [2, 128, 4096], P(None, ('dp', 'tp'))
- output 3: float32 [4096, 14336], P('dp', 'tp')
- output 4: float32 [4096, 14336], P('dp', 'tp')
- output 5: float32 [14336, 4096], P('tp', 'dp')
All inputs are finite; a program needn't handle non-finite values.
Results may differ from a plain program's by a relative error of at most 0.001.
Values are sent between devices in bfloat16 or wider.
A program may use at most 1 GiB of HBM per device.

v0:
```python
import jax
import jax.numpy as jnp
from jax import lax
from jax.sharding import PartitionSpec as P


def gate_grads(grad_h, gate_pre, up_pre, sig_gate, act_gate):
    grad_gate = grad_h * up_pre * sig_gate * (1.0 + gate_pre * (1.0 - sig_gate))
    grad_up = grad_h * act_gate
    return grad_gate.astype(jnp.bfloat16), grad_up.astype(jnp.bfloat16)


def solution(mesh):
    data_size = mesh.shape["dp"]
    model_size = mesh.shape["tp"]
    row_spec = P(None, ("dp", "tp"), None)
    in_specs = (row_spec, P("dp", "tp"), P("dp", "tp"), P("tp", "dp"), row_spec)
    out_specs = (row_spec, row_spec, P("dp", "tp"), P("dp", "tp"), P("tp", "dp"))

    def token_columns(rows_loc):
        spread = lax.all_to_all(rows_loc, "dp", split_axis=1, concat_axis=0, tiled=True)
        gathered = lax.all_gather(spread, "tp", axis=0)
        return gathered.reshape(model_size, data_size, -1, gathered.shape[-1])

    def reduce_data(part_sum):
        return lax.psum_scatter(part_sum, "dp", scatter_dimension=1, tiled=True)[:, 0]

    def to_rows(part_sum):
        reduced = lax.psum_scatter(part_sum, "tp", scatter_dimension=0, tiled=True)[0]
        return lax.all_to_all(reduced, "dp", split_axis=0, concat_axis=2, tiled=True)[0]

    def local_step(x_loc, w_gate_loc, w_up_loc, w_down_loc, dy_loc):
        y_list = []
        dx_list = []
        for micro_idx in range(x_loc.shape[0]):
            x_cols = token_columns(x_loc[micro_idx])
            gate_pre = reduce_data(jnp.einsum("tkrd,df->tkrf", x_cols, w_gate_loc, preferred_element_type=jnp.float32))
            up_pre = reduce_data(jnp.einsum("tkrd,df->tkrf", x_cols, w_up_loc, preferred_element_type=jnp.float32))
            sig_gate = jax.nn.sigmoid(gate_pre)
            act_gate = gate_pre * sig_gate
            hidden = (act_gate * up_pre).astype(jnp.bfloat16)
            hidden_all = lax.all_gather(hidden, "dp", axis=1)
            out_sum = to_rows(jnp.einsum("tkrf,fd->tkrd", hidden_all, w_down_loc, preferred_element_type=jnp.float32))
            y_list.append((x_loc[micro_idx].astype(jnp.float32) + out_sum).astype(jnp.bfloat16))
            dy_cols = token_columns(dy_loc[micro_idx])
            grad_h = reduce_data(jnp.einsum("tkrd,fd->tkrf", dy_cols, w_down_loc, preferred_element_type=jnp.float32))
            grad_gate, grad_up = gate_grads(grad_h, gate_pre, up_pre, sig_gate, act_gate)
            gate_all = lax.all_gather(grad_gate, "dp", axis=1)
            up_all = lax.all_gather(grad_up, "dp", axis=1)
            dx_part = jnp.einsum("tkrf,df->tkrd", gate_all, w_gate_loc, preferred_element_type=jnp.float32) + jnp.einsum("tkrf,df->tkrd", up_all, w_up_loc, preferred_element_type=jnp.float32)
            dx_list.append((dy_loc[micro_idx].astype(jnp.float32) + to_rows(dx_part)).astype(jnp.bfloat16))
            dw_gate = jnp.einsum("tkrd,tkrf->df", x_cols, gate_all, preferred_element_type=jnp.float32)
            dw_up = jnp.einsum("tkrd,tkrf->df", x_cols, up_all, preferred_element_type=jnp.float32)
            dw_down = jnp.einsum("tkrf,tkrd->fd", hidden_all, dy_cols, preferred_element_type=jnp.float32)
            if micro_idx == 0:
                gate_sum, up_sum, down_sum = dw_gate, dw_up, dw_down
            else:
                gate_sum = gate_sum + dw_gate
                up_sum = up_sum + dw_up
                down_sum = down_sum + dw_down
        return jnp.stack(y_list), jnp.stack(dx_list), gate_sum, up_sum, down_sum

    return jax.shard_map(local_step, mesh=mesh, in_specs=in_specs, out_specs=out_specs, check_vma=False)
```

profile of v0, /device:TPU:0, one launch (start us, length us, event | category | flops | bytes accessed | tf_op | source)
XLA Modules:
  0.0 498.4 jit_solution(5067558024092261591)
XLA Ops:
  8.7 4.5 all-to-all-start.2
  20.4 9.8 %all_gather.52 = bf16[4,32,1024]{2,1,0:T(8,128)(2,1)S(1)} all-gather(bf16[1,32,1024]{2,1,0:T(8,128)(2,1)S(1)} %bitcast.174), channel_id=1, replica_groups=mesh['tp'=4,'dp'=4] {'tp'}, dimensions={0}, use_global_device_ids=true | all-gather | bytes 327680 | tf_op jit(solution)/shard_map/all_gather | solution.py:22
  30.2 5.4 %fusion.14 = f32[4,4,8,3584]{3,2,1,0:T(8,128)} fusion(bf16[1024,3584]{1,0:T(8,128)(2,1)} %param.7, bf16[4,32,1024]{2,1,0:T(8,128)(2,1)S(1)} %all_gather.52), kind=kOutput, calls=%fused_computation.17 | convolution fusion | flops 939524096 | bytes 9437184 | tf_op jit(solution)/shard_map/tkrd,df->tkrf/dot_general | solution.py:38
  41.3 9.3 %all_gather.49 = bf16[4,32,1024]{2,1,0:T(8,128)(2,1)S(1)} all-gather(bf16[1,32,1024]{2,1,0:T(8,128)(2,1)S(1)} %bitcast.175), channel_id=1, replica_groups=mesh['tp'=4,'dp'=4] {'tp'}, dimensions={0}, use_global_device_ids=true | all-gather | bytes 327680 | tf_op jit(solution)/shard_map/all_gather | solution.py:22
  50.6 5.5 %fusion.16 = f32[4,4,8,3584]{3,2,1,0:T(8,128)} fusion(bf16[1024,3584]{1,0:T(8,128)(2,1)} %param.7, bf16[4,32,1024]{2,1,0:T(8,128)(2,1)S(1)} %all_gather.49), kind=kOutput, calls=%fused_computation.19 | convolution fusion | flops 939524096 | bytes 9437184 | tf_op jit(solution)/shard_map/tkrd,df->tkrf/dot_general | solution.py:38
  61.9 8.0 %all_gather.59 = bf16[4,32,1024]{2,1,0:T(8,128)(2,1)S(1)} all-gather(bf16[1,32,1024]{2,1,0:T(8,128)(2,1)S(1)} %bitcast.173), channel_id=1, replica_groups=mesh['tp'=4,'dp'=4] {'tp'}, dimensions={0}, use_global_device_ids=true | all-gather | bytes 327680 | tf_op jit(solution)/shard_map/all_gather | solution.py:22
  69.9 9.0 %all_gather.55 = bf16[4,32,1024]{2,1,0:T(8,128)(2,1)S(1)} all-gather(bf16[1,32,1024]{2,1,0:T(8,128)(2,1)S(1)} %bitcast.176), channel_id=1, replica_groups=mesh['tp'=4,'dp'=4] {'tp'}, dimensions={0}, use_global_device_ids=true | all-gather | bytes 327680 | tf_op jit(solution)/shard_map/all_gather | solution.py:22
  78.9 6.9 %fusion.2 = f32[4,4,8,3584]{3,2,1,0:T(8,128)} fusion(bf16[3584,1024]{1,0:T(8,128)(2,1)} %param.8, bf16[4,32,1024]{2,1,0:T(8,128)(2,1)S(1)} %all_gather.59), kind=kOutput, calls=%fused_computation.5 | convolution fusion | flops 939524096 | bytes 9437184 | tf_op jit(solution)/shard_map/tkrd,fd->tkrf/dot_general | solution.py:46
  85.8 6.8 %fusion.4 = f32[4,4,8,3584]{3,2,1,0:T(8,128)} fusion(bf16[3584,1024]{1,0:T(8,128)(2,1)} %param.8, bf16[4,32,1024]{2,1,0:T(8,128)(2,1)S(1)} %all_gather.55), kind=kOutput, calls=%fused_computation.7 | convolution fusion | flops 939524096 | bytes 9437184 | tf_op jit(solution)/shard_map/tkrd,fd->tkrf/dot_general | solution.py:46
  93.9 190.8 %all-reduce.13.cloned.1.call-done = (f32[4,4,8,3584]{3,2,1,0:T(8,128)}, f32[4,4,8,3584]{3,2,1,0:T(8,128)}, f32[4,4,8,3584]{3,2,1,0:T(8,128)}, f32[4,4,8,3584]{3,...) async-done(((f32[4,4,8,3584]{3,2,1,0:T(8,128)}, f32[4,4,8,3584]{3,2,1,0:T(8,128)}, f32[4,4,8,3584]{3,2,1,0:T(8,128)}, f32[4,4,8,3584]{3,2,1,0:T(8,128)}, ...) | async-done | bytes 11010064
  287.6 8.8 %all_gather.57 = bf16[4,4,8,3584]{3,2,1,0:T(8,128)(2,1)S(1)} all-gather(bf16[4,1,8,3584]{3,2,1,0:T(8,128)(2,1)S(1)} %get-tuple-element.23), channel_id=1, replica_groups=mesh['tp'=4,'dp'=4] {'dp'}, dimensions={1}, use_global_device_ids=true | all-gather | bytes 1146880 | tf_op jit(solution)/shard_map/all_gather | solution.py:49
  296.4 6.5 %fusion.12 = f32[4,4,8,1024]{3,2,1,0:T(8,128)} fusion(bf16[4,4,8,3584]{3,2,1,0:T(8,128)(2,1)S(1)} %all_gather.57, bf16[1024,3584]{1,0:T(8,128)(2,1)} %param.7), kind=kOutput, calls=%fused_computation.15 | convolution fusion | flops 939524096 | bytes 8781824 | tf_op jit(solution)/shard_map/tkrf,df->tkrd/dot_general | solution.py:50
  302.9 7.6 %fusion.36 = f32[3584,1024,1,1]{1,0,3,2:T(8,128)} fusion(bf16[4,4,8,3584]{3,2,1,0:T(8,128)(2,1)S(1)} %all_gather.57, bf16[4,32,1024]{2,1,0:T(8,128)(2,1)S(1)} %copy-done.4), kind=kOutput, calls=%fused_computation.35 | convolution fusion | flops 939524096 | bytes 15859712 | tf_op jit(solution)/shard_map/tkrd,tkrf->df/dot_general | solution.py:53
  310.5 9.4 %all_gather.50 = bf16[4,4,8,3584]{3,2,1,0:T(8,128)(2,1)S(1)} all-gather(bf16[4,1,8,3584]{3,2,1,0:T(8,128)(2,1)S(1)} %get-tuple-element.22), channel_id=1, replica_groups=mesh['tp'=4,'dp'=4] {'dp'}, dimensions={1}, use_global_device_ids=true | all-gather | bytes 1146880 | tf_op jit(solution)/shard_map/all_gather | solution.py:42
  322.8 9.0 %fusion.33 = f32[3584,1024,1,1]{1,0,3,2:T(8,128)} fusion(bf16[4,4,8,3584]{3,2,1,0:T(8,128)(2,1)} %copy-done.2, bf16[4,32,1024]{2,1,0:T(8,128)(2,1)} %copy-done.8), kind=kOutput, calls=%fused_computation.32 | convolution fusion | flops 939524096 | bytes 15859712 | tf_op jit(solution)/shard_map/tkrf,tkrd->fd/dot_general | solution.py:54
  335.1 9.4 %all_gather.53 = bf16[4,4,8,3584]{3,2,1,0:T(8,128)(2,1)} all-gather(bf16[4,1,8,3584]{3,2,1,0:T(8,128)(2,1)S(1)} %get-tuple-element.25), channel_id=1, replica_groups=mesh['tp'=4,'dp'=4] {'dp'}, dimensions={1}, use_global_device_ids=true | all-gather | bytes 1146880 | tf_op jit(solution)/shard_map/all_gather | solution.py:42
  344.5 9.4 %all_gather.56 = bf16[4,4,8,3584]{3,2,1,0:T(8,128)(2,1)S(1)} all-gather(bf16[4,1,8,3584]{3,2,1,0:T(8,128)(2,1)} %get-tuple-element.21), channel_id=1, replica_groups=mesh['tp'=4,'dp'=4] {'dp'}, dimensions={1}, use_global_device_ids=true | all-gather | bytes 1146880 | tf_op jit(solution)/shard_map/all_gather | solution.py:48
  353.9 8.6 %fusion.39 = f32[3584,1024,1,1]{1,0,3,2:T(8,128)} fusion(bf16[4,4,8,3584]{3,2,1,0:T(8,128)(2,1)S(1)} %all_gather.56, bf16[4,32,1024]{2,1,0:T(8,128)(2,1)} %copy-done.3), kind=kOutput, calls=%fused_computation.38 | convolution fusion | flops 939524096 | bytes 15859712 | tf_op jit(solution)/shard_map/tkrd,tkrf->df/dot_general | solution.py:52
  365.8 9.4 %all_gather.61 = bf16[4,4,8,3584]{3,2,1,0:T(8,128)(2,1)S(1)} all-gather(bf16[4,1,8,3584]{3,2,1,0:T(8,128)(2,1)} %get-tuple-element.26), channel_id=1, replica_groups=mesh['tp'=4,'dp'=4] {'dp'}, dimensions={1}, use_global_device_ids=true | all-gather | bytes 1146880 | tf_op jit(solution)/shard_map/all_gather | solution.py:49
  375.2 9.6 %all_gather.60 = bf16[4,4,8,3584]{3,2,1,0:T(8,128)(2,1)S(1)} all-gather(bf16[4,1,8,3584]{3,2,1,0:T(8,128)(2,1)} %get-tuple-element.24), channel_id=1, replica_groups=mesh['tp'=4,'dp'=4] {'dp'}, dimensions={1}, use_global_device_ids=true | all-gather | bytes 1146880 | tf_op jit(solution)/shard_map/all_gather | solution.py:48
  384.9 5.3 %fusion.6 = f32[4,4,8,1024]{3,2,1,0:T(8,128)} fusion(bf16[4,4,8,3584]{3,2,1,0:T(8,128)(2,1)} %all_gather.53, bf16[3584,1024]{1,0:T(8,128)(2,1)} %param.8), kind=kOutput, calls=%fused_computation.9 | convolution fusion | flops 939524096 | bytes 8781824 | tf_op jit(solution)/shard_map/tkrf,fd->tkrd/dot_general | solution.py:43
  390.2 12.5 %fusion = f32[1024,3584]{0,1:T(8,128)} fusion(f32[3584,1024,1,1]{1,0,3,2:T(8,128)} %fusion.36, bf16[4,4,8,3584]{3,2,1,0:T(8,128)(2,1)S(1)} %all_gather.61, bf16[4,32,1024]{2,1,0:T(8,128)(2,1)S(1)} %all_gather.52), kind=kOutput, calls=%fused_computation.2 | convolution fusion | flops 943194112 | bytes 30539776 | tf_op jit(solution)/shard_map/tkrd,tkrf->df/dot_general | solution.py:53
  402.7 5.6 %fusion.10 = f32[4,4,8,1024]{3,2,1,0:T(8,128)S(1)} fusion(bf16[4,4,8,3584]{3,2,1,0:T(8,128)(2,1)S(1)} %all_gather.61, bf16[1024,3584]{1,0:T(8,128)(2,1)} %param.7), kind=kOutput, calls=%fused_computation.13 | convolution fusion | flops 939524096 | bytes 8781824 | tf_op jit(solution)/shard_map/tkrf,df->tkrd/dot_general | solution.py:50
  408.4 12.8 %fusion.1 = f32[1024,3584]{0,1:T(8,128)} fusion(f32[3584,1024,1,1]{1,0,3,2:T(8,128)} %fusion.39, bf16[4,4,8,3584]{3,2,1,0:T(8,128)(2,1)S(1)} %all_gather.60, bf16[4,32,1024]{2,1,0:T(8,128)(2,1)S(1)} %all_gather.52), kind=kOutput, calls=%fused_computation.4 | convolution fusion | flops 943194112 | bytes 30539776 | tf_op jit(solution)/shard_map/tkrd,tkrf->df/dot_general | solution.py:52
  421.1 3.5 all-to-all-start.1
  424.6 6.4 %fusion.29 = f32[4,4,8,1024]{3,2,1,0:T(8,128)} fusion(f32[4,4,8,1024]{3,2,1,0:T(8,128)S(1)} %fusion.10, bf16[4,4,8,3584]{3,2,1,0:T(8,128)(2,1)S(1)} %all_gather.60, bf16[1024,3584]{1,0:T(8,128)(2,1)} %param.6), kind=kOutput, calls=%fused_computation.30 | convolution fusion | flops 939655168 | bytes 9306112 | tf_op jit(solution)/shard_map/tkrf,df->tkrd/dot_general | solution.py:50
  431.1 3.3 all-to-all-start.3
  434.4 12.8 %bitcast_add_fusion = f32[3584,1024]{1,0:T(8,128)} fusion(f32[3584,1024,1,1]{1,0,3,2:T(8,128)} %fusion.33, bf16[4,4,8,3584]{3,2,1,0:T(8,128)(2,1)S(1)} %copy-done.1, bf16[4,32,1024]{2,1,0:T(8,128)(2,1)S(1)} %copy-done.7), kind=kOutput, calls=%fused_computation | convolution fusion | flops 943194112 | bytes 30539776 | tf_op jit(solution)/shard_map/tkrf,tkrd->fd/dot_general | solution.py:54
  447.2 14.3 %copy.36 = f32[1024,3584]{1,0:T(8,128)} copy(f32[1024,3584]{0,1:T(8,128)} %fusion.1) | data formatting | bytes 29360128
  461.5 14.3 %copy.37 = f32[1024,3584]{1,0:T(8,128)} copy(f32[1024,3584]{0,1:T(8,128)} %fusion) | data formatting | bytes 29360128
  479.2 4.3 all-to-all-done.5
  487.5 3.7 all-to-all-done.7
  (77 shorter events, 42.0 us)
Async XLA Ops:
  8.7 8.4 %all-to-all-start.2 = ((bf16[8,4,1024]{2,0,1:T(8,128)(2,1)}), bf16[8,4,1024]{2,0,1:T(8,128)(2,1)S(1)}, u32[]{:S(2)}, u32[]{:S(2)}) async-start(bf16[8,4,1024]{2,0,1:T(8,128)(2,1)} %bitcast.14), calls=%async_computation.2 | async-start | bytes 131072 | tf_op jit(solution)/shard_map/all_to_all | solution.py:21
  17.1 20.9 %all-to-all-start = ((bf16[8,4,1024]{2,0,1:T(8,128)(2,1)}), bf16[8,4,1024]{2,0,1:T(8,128)(2,1)S(1)}, u32[]{:S(2)}, u32[]{:S(2)}) async-start(bf16[8,4,1024]{2,0,1:T(8,128)(2,1)} %bitcast), calls=%async_computation | async-start | bytes 131072 | tf_op jit(solution)/shard_map/all_to_all | solution.py:21
  20.4 15.3 %copy-start = (bf16[1024,3584]{1,0:T(8,128)(2,1)S(1)}, bf16[1024,3584]{1,0:T(8,128)(2,1)}, u32[]{:S(2)}) copy-start(bf16[1024,3584]{1,0:T(8,128)(2,1)} %param.6) | copy-start | bytes 22020100
  35.7 20.5 %slice-start = ((s8[7340032]{0:T(1024)(128)(4,1)}), s8[3145728]{0:T(1024)(128)(4,1)S(1)}, s32[]{:S(2)}) async-start(s8[7340032]{0:T(1024)(128)(4,1)} %bitcast.163), calls=%async_computation.17 | async-start | bytes 6291456
  38.0 20.5 %all-to-all-start.6 = ((bf16[8,4,1024]{2,0,1:T(8,128)(2,1)}), bf16[8,4,1024]{2,0,1:T(8,128)(2,1)S(1)}, u32[]{:S(2)}, u32[]{:S(2)}) async-start(bf16[8,4,1024]{2,0,1:T(8,128)(2,1)} %bitcast.177), calls=%async_computation.6 | async-start | bytes 131072 | tf_op jit(solution)/shard_map/all_to_all | solution.py:21
  41.3 14.8 %slice-start.1 = ((s8[7340032]{0:T(1024)(128)(4,1)}), s8[4194304]{0:T(1024)(128)(4,1)S(1)}, s32[]{:S(2)}) async-start(s8[7340032]{0:T(1024)(128)(4,1)} %bitcast.163), calls=%async_computation.18 | async-start | bytes 8388608
  50.6 5.5 %copy-start.3 = (bf16[4,32,1024]{2,1,0:T(8,128)(2,1)}, bf16[4,32,1024]{2,1,0:T(8,128)(2,1)S(1)}, u32[]{:S(2)}) copy-start(bf16[4,32,1024]{2,1,0:T(8,128)(2,1)S(1)} %all_gather.49) | copy-start | bytes 786436
  58.5 11.3 %all-to-all-start.4 = ((bf16[8,4,1024]{2,0,1:T(8,128)(2,1)}), bf16[8,4,1024]{2,0,1:T(8,128)(2,1)S(1)}, u32[]{:S(2)}, u32[]{:S(2)}) async-start(bf16[8,4,1024]{2,0,1:T(8,128)(2,1)} %bitcast.25), calls=%async_computation.4 | async-start | bytes 131072 | tf_op jit(solution)/shard_map/all_to_all | solution.py:21
  61.8 222.9 %all-reduce.13.cloned.1.call-start = ((), (), s32[]{:S(2)}) async-start(), calls=%async_computation.16 | async-start | bytes 22020096
  69.9 22.8 %copy-start.6 = (bf16[4,32,1024]{2,1,0:T(8,128)(2,1)}, bf16[4,32,1024]{2,1,0:T(8,128)(2,1)S(1)}, u32[]{:S(2)}) copy-start(bf16[4,32,1024]{2,1,0:T(8,128)(2,1)S(1)} %all_gather.59) | copy-start | bytes 786436
  78.9 13.8 %copy-start.8 = (bf16[4,32,1024]{2,1,0:T(8,128)(2,1)}, bf16[4,32,1024]{2,1,0:T(8,128)(2,1)S(1)}, u32[]{:S(2)}) copy-start(bf16[4,32,1024]{2,1,0:T(8,128)(2,1)S(1)} %all_gather.55) | copy-start | bytes 786436
  92.7 0.7 copy-start.11
  92.7 328.4 %reduce-scatter.19.cloned.1.call-start = ((), (), s32[]{:S(2)}) async-start(), calls=%async_computation.12 | async-start | bytes 655360
  287.6 15.3 %copy-start.4 = (bf16[4,32,1024]{2,1,0:T(8,128)(2,1)S(1)}, bf16[4,32,1024]{2,1,0:T(8,128)(2,1)}, u32[]{:S(2)}) copy-start(bf16[4,32,1024]{2,1,0:T(8,128)(2,1)} %copy-done.3) | copy-start | bytes 786436
  296.4 24.4 %slice-start.4 = ((s8[7340032]{0:T(1024)(128)(4,1)}), s8[3145728]{0:T(1024)(128)(4,1)S(1)}, s32[]{:S(2)}) async-start(s8[7340032]{0:T(1024)(128)(4,1)} %bitcast.167), calls=%async_computation.21 | async-start | bytes 6291456
  302.9 17.9 %slice-start.5 = ((s8[7340032]{0:T(1024)(128)(4,1)}), s8[4194304]{0:T(1024)(128)(4,1)S(1)}, s32[]{:S(2)}) async-start(s8[7340032]{0:T(1024)(128)(4,1)} %bitcast.167), calls=%async_computation.22 | async-start | bytes 8388608
  319.9 0.9 copy-start.2
  322.8 39.7 %slice-start.2 = ((s8[7340032]{0:T(1024)(128)(4,1)}), s8[3145728]{0:T(1024)(128)(4,1)S(1)}, s32[]{:S(2)}) async-start(s8[7340032]{0:T(1024)(128)(4,1)} %bitcast.165), calls=%async_computation.19 | async-start | bytes 6291456
  331.8 99.3 %reduce-scatter.21.cloned.1.call-start = ((), (), s32[]{:S(2)}) async-start(), calls=%async_computation.13 | async-start | bytes 655360
  331.8 30.7 %slice-start.3 = ((s8[7340032]{0:T(1024)(128)(4,1)}), s8[4194304]{0:T(1024)(128)(4,1)S(1)}, s32[]{:S(2)}) async-start(s8[7340032]{0:T(1024)(128)(4,1)} %bitcast.165), calls=%async_computation.20 | async-start | bytes 8388608
  353.9 8.6 %copy-start.5 = (f32[4,4,8,1024]{3,2,1,0:T(8,128)S(1)}, f32[4,4,8,1024]{3,2,1,0:T(8,128)}, u32[]{:S(2)}) copy-start(f32[4,4,8,1024]{3,2,1,0:T(8,128)} %fusion.12) | copy-start | bytes 1572868
  390.2 85.6 %reduce-scatter.23.cloned.1.call-start = ((), (), s32[]{:S(2)}) async-start(), calls=%async_computation.14 | async-start | bytes 655360
  421.1 13.3 %copy-start.1 = (bf16[4,4,8,3584]{3,2,1,0:T(8,128)(2,1)S(1)}, bf16[4,4,8,3584]{3,2,1,0:T(8,128)(2,1)}, u32[]{:S(2)}) copy-start(bf16[4,4,8,3584]{3,2,1,0:T(8,128)(2,1)} %all_gather.53) | copy-start | bytes 2752516
  421.1 13.3 %copy-start.7 = (bf16[4,32,1024]{2,1,0:T(8,128)(2,1)S(1)}, bf16[4,32,1024]{2,1,0:T(8,128)(2,1)}, u32[]{:S(2)}) copy-start(bf16[4,32,1024]{2,1,0:T(8,128)(2,1)} %copy-done.6) | copy-start | bytes 786436
  421.1 10.0 %all-to-all-start.1 = ((f32[4,8,1024]{2,1,0:T(8,128)}), f32[4,8,1024]{2,1,0:T(8,128)S(1)}, u32[]{:S(2)}, u32[]{:S(2)}) async-start(f32[4,8,1024]{2,1,0:T(8,128)} %bitcast.178), calls=%async_computation.1 | async-start | bytes 262144 | tf_op jit(solution)/shard_map/all_to_all | solution.py:30
  424.6 54.6 %reduce-scatter.25.cloned.1.call-start = ((), (), s32[]{:S(2)}) async-start(), calls=%async_computation.15 | async-start | bytes 655360
  431.1 44.7 %all-to-all-start.3 = ((f32[4,8,1024]{2,1,0:T(8,128)}), f32[4,8,1024]{2,1,0:T(8,128)S(1)}, u32[]{:S(2)}, u32[]{:S(2)}) async-start(f32[4,8,1024]{2,1,0:T(8,128)} %bitcast.180), calls=%async_computation.3 | async-start | bytes 262144 | tf_op jit(solution)/shard_map/all_to_all | solution.py:30
  461.5 17.7 %copy-start.9 = (bf16[2,8,4096]{2,1,0:T(8,128)(2,1)S(1)}, bf16[2,8,4096]{2,1,0:T(8,128)(2,1)}, u32[]{:S(2)}) copy-start(bf16[2,8,4096]{2,1,0:T(8,128)(2,1)} %param.5) | copy-start | bytes 393220
  461.5 29.7 %copy-start.10 = (bf16[2,8,4096]{2,1,0:T(8,128)(2,1)S(1)}, bf16[2,8,4096]{2,1,0:T(8,128)(2,1)}, u32[]{:S(2)}) copy-start(bf16[2,8,4096]{2,1,0:T(8,128)(2,1)} %param.9) | copy-start | bytes 393220
  475.8 7.7 %all-to-all-start.5 = ((f32[4,8,1024]{2,1,0:T(8,128)}), f32[4,8,1024]{2,1,0:T(8,128)S(1)}, u32[]{:S(2)}, u32[]{:S(2)}) async-start(f32[4,8,1024]{2,1,0:T(8,128)} %bitcast.179), calls=%async_computation.5 | async-start | bytes 262144 | tf_op jit(solution)/shard_map/all_to_all | solution.py:30
  483.5 7.7 %all-to-all-start.7 = ((f32[4,8,1024]{2,1,0:T(8,128)}), f32[4,8,1024]{2,1,0:T(8,128)S(1)}, u32[]{:S(2)}, u32[]{:S(2)}) async-start(f32[4,8,1024]{2,1,0:T(8,128)} %bitcast.181), calls=%async_computation.7 | async-start | bytes 262144 | tf_op jit(solution)/shard_map/all_to_all | solution.py:30
Sparse Core Ops, SparseCore 0:
  92.8 191.8 all-reduce.12
  331.9 22.1 reduce-scatter.18
  390.3 22.1 reduce-scatter.20
  415.2 21.3 reduce-scatter.22
  439.2 21.3 reduce-scatter.24
where the time goes:
time: 500 us; the launch traced here: 498 us
  waiting for transfers between devices  201 us (40%)
  matrix products  122 us (24%)
  blocking collectives  92 us (18%)
  local copies, waits for them, and re-layouts  33.8 us (7%)
  starting transfers between devices  28 us (6%)
  between operations  14 us (3%)
  other arithmetic  7.55 us (2%)
    unnamed x10, waiting for transfers between devices  191 us
    all_gather x4, blocking collectives, token_columns(): gathered = lax.all_gather(spread, 'tp', axis=0)  36 us
    unnamed x39, local copies, waits for them, and re-layouts  30.7 us
    dot_general x2, matrix products, local_step(): jnp.einsum('tkrf,tkrd->fd', hidden_all, dy_cols, preferred_element_type=j...  21.7 us
    dot_general x2, matrix products, local_step(): jnp.einsum('tkrd,tkrf->df', x_cols, gate_all, preferred_element_type=jnp....  21.3 us
    dot_general x2, matrix products, local_step(): jnp.einsum('tkrd,tkrf->df', x_cols, up_all, preferred_element_type=jnp.fl...  20.1 us
    all_gather x2, blocking collectives, local_step(): gate_all = lax.all_gather(grad_gate, 'dp', axis=1)  19 us
    all_gather x2, blocking collectives, local_step(): hidden_all = lax.all_gather(hidden, 'dp', axis=1)  18.8 us
  transfers between devices with their start and end apart: 13, of which 4 were waited for; matrix products, arithmetic and copies ran while one was open for 24% of the time, Pallas kernels for 0%

commit v1 on v0

v1 whole, which is shorter than its diff:
```python
import jax
import jax.numpy as jnp
from jax import lax
from jax.experimental import pallas as pl
from jax.experimental.pallas import tpu as pltpu
from jax.sharding import PartitionSpec as P

MESH = pl.DeviceIdType.MESH
F32 = jnp.float32
BF16 = jnp.bfloat16
GROUPS = 4
SLOTS = 4
FINAL_LAG = 4
FORWARD_LAG = 7
BACK_LAG = 8


def dot(lhs, rhs):
    return lax.dot_general(lhs, rhs, (((1,), (0,)), ((), ())), preferred_element_type=F32)


def dot_t(lhs, rhs):
    return lax.dot_general(lhs, rhs, (((1,), (1,)), ((), ())), preferred_element_type=F32)


def make_kernel(chunks, width):
    total = GROUPS * chunks
    rest = total - chunks

    def kernel(x_ref, dy_ref, wg_hbm, wu_hbm, wd_hbm,
               y_out, dx_out, h_out, da_out, db_out, xc_out, dyc_out,
               wg, wu, wd, cols, part, near, far, hid, acc, acc_in, tail, rows,
               w_sem, first_send, first_recv, spread_send, spread_recv,
               near_send, near_recv, far_send, far_recv,
               hc_send, hc_recv, hx_send, hx_recv, hf_send, hf_recv,
               acc_send, acc_recv, tail_send, tail_recv, out_sem, cols_sem, row_sem):
        tp = lax.axis_index("tp")
        dp = lax.axis_index("dp")
        z, y = tp // 2, tp % 2
        x, core = dp // 2, dp % 2
        ox, oc = 1 - x, 1 - core
        core_peer = {"tp": tp, "dp": x * 2 + oc}
        x_peer = {"tp": tp, "dp": ox * 2 + core}
        mine = core * 2 + x
        depth = cols.shape[-1]

        def tp_peer(group):
            return {"tp": ((z + group // 2) % 2) * 2 + (y + group % 2) % 2, "dp": dp}

        def dp_peer(k):
            px, pc = (x + k // 2) % 2, (core + k % 2) % 2
            return px * 2 + pc, pc * 2 + px

        def weight_copies(c):
            span = pl.ds(pl.multiple_of(c * width, width), width)
            return (pltpu.make_async_copy(wg_hbm.at[:, span], wg.at[c], w_sem.at[c, 0]),
                    pltpu.make_async_copy(wu_hbm.at[:, span], wu.at[c], w_sem.at[c, 1]),
                    pltpu.make_async_copy(wd_hbm.at[span], wd.at[c], w_sem.at[c, 2]))

        def remote(src, dst, send, recv, device):
            return pltpu.make_async_remote_copy(src_ref=src, dst_ref=dst, send_sem=send, recv_sem=recv,
                                                device_id=device, device_id_type=MESH)

        def first_copy(kind, k):
            peer, _ = dp_peer(k)
            src = (x_ref, dy_ref)[kind].at[:, pl.ds(pl.multiple_of(peer * depth, depth), depth)]
            return remote(src, cols.at[0, kind, mine], first_send.at[kind, k - 1], first_recv.at[kind, k - 1], {"tp": tp, "dp": peer})

        def spread_copy(group):
            return remote(cols.at[0], cols.at[group], spread_send.at[group - 1], spread_recv.at[group - 1], tp_peer(group))

        def near_copy(i):
            return remote(part.at[i, pl.ds(oc * 2, 2)], near.at[i], near_send.at[i], near_recv.at[i], core_peer)

        def far_copy(i):
            return remote(near.at[i, ox], far.at[i], far_send.at[i], far_recv.at[i], x_peer)

        def hc_copy(i):
            here = hid.at[i, :, mine]
            return remote(here, here, hc_send.at[i], hc_recv.at[i], core_peer)

        def hx_copy(i):
            here = hid.at[i, :, mine]
            return remote(here, here, hx_send.at[i], hx_recv.at[i], x_peer)

        def hf_copy(i):
            there = hid.at[i, :, core * 2 + ox]
            return remote(there, there, hf_send.at[i], hf_recv.at[i], core_peer)

        def acc_copy(group):
            return remote(acc.at[group], acc_in.at[group - 1], acc_send.at[group - 1], acc_recv.at[group - 1], tp_peer(group))

        def out_copies(i):
            group, c = i // chunks, i % chunks
            span = pl.ds(pl.multiple_of(c * width, width), width)
            return [pltpu.make_async_copy(hid.at[i, k], ref.at[group, :, :, span], out_sem.at[i, k])
                    for k, ref in enumerate((h_out, da_out, db_out))]

        def cols_copies(group):
            return [pltpu.make_async_copy(cols.at[group, k], ref.at[group], cols_sem.at[group, k])
                    for k, ref in enumerate((xc_out, dyc_out))]

        def tail_copy(kind, k):
            peer, slot = dp_peer(k)
            dst = rows.at[kind, :, pl.ds(pl.multiple_of(dp * depth, depth), depth)]
            return remote(tail.at[kind, slot], dst, tail_send.at[kind, k - 1], tail_recv.at[kind, k - 1], {"tp": tp, "dp": peer})

        for c in range(chunks):
            for copy in weight_copies(c):
                copy.start()

        barrier = pltpu.get_barrier_semaphore()
        for k in range(1, 4):
            pl.semaphore_signal(barrier, inc=1, device_id={"tp": tp, "dp": dp_peer(k)[0]}, device_id_type=MESH)
            pl.semaphore_signal(barrier, inc=1, device_id=tp_peer(k), device_id_type=MESH)
        pl.semaphore_wait(barrier, 6)

        for k in (2, 3, 1):
            for kind in range(2):
                first_copy(kind, k).start()
        own = pl.ds(pl.multiple_of(dp * depth, depth), depth)
        cols[0, 0, mine] = x_ref[:, own]
        cols[0, 1, mine] = dy_ref[:, own]
        acc[...] = jnp.zeros_like(acc)
        for k in (1, 2, 3):
            for kind in range(2):
                first_copy(kind, k).wait_recv()
        for group in (1, 2, 3):
            spread_copy(group).start()

        def products(i):
            group, c = i // chunks, i % chunks

            @pl.when(group == 0)
            def _():
                for copy in weight_copies(c):
                    copy.wait()

            @pl.when(jnp.logical_and(group > 0, c == 0))
            def _():
                spread_copy(group).wait_recv()

            x_rows = cols[group, 0].reshape(SLOTS * 16, depth)
            dy_rows = cols[group, 1].reshape(SLOTS * 16, depth)
            for k, value in enumerate((dot(x_rows, wg[c]), dot(x_rows, wu[c]), dot_t(dy_rows, wd[c]))):
                for slot in range(SLOTS):
                    part[i, slot, k] = value[slot * 16:(slot + 1) * 16]
            near_copy(i).start()

        def half_sum(i):
            near_copy(i).wait_recv()
            near[i, ox] = near[i, ox] + part[i, core * 2 + ox]
            far_copy(i).start()

        def activations(i):
            far_copy(i).wait_recv()
            gate = part[i, mine, 0] + near[i, x, 0] + far[i, 0]
            up = part[i, mine, 1] + near[i, x, 1] + far[i, 1]
            grad = part[i, mine, 2] + near[i, x, 2] + far[i, 2]
            sig = jax.nn.sigmoid(gate)
            act = gate * sig
            hid[i, 0, mine] = (act * up).astype(BF16)
            hid[i, 1, mine] = (grad * up * sig * (1.0 + gate * (1.0 - sig))).astype(BF16)
            hid[i, 2, mine] = (grad * act).astype(BF16)
            hc_copy(i).start()

        def back(i):
            group, c = i // chunks, i % chunks
            hc_copy(i).wait_recv()
            hf_copy(i).wait_recv()
            for copy in out_copies(i):
                copy.start()
            h_rows = hid[i, 0].reshape(SLOTS * 16, width)
            da_rows = hid[i, 1].reshape(SLOTS * 16, width)
            db_rows = hid[i, 2].reshape(SLOTS * 16, width)
            acc[group, 0] += dot(h_rows, wd[c]).reshape(SLOTS, 16, depth)
            acc[group, 1] += (dot_t(da_rows, wg[c]) + dot_t(db_rows, wu[c])).reshape(SLOTS, 16, depth)

            @pl.when(jnp.logical_and(group > 0, c == chunks - 1))
            def _():
                acc_copy(group).start()

        def step(s, carry):
            @pl.when(s < total)
            def _():
                products(s)

            @pl.when(jnp.logical_and(s >= 1, s < total + 1))
            def _():
                half_sum(s - 1)

            @pl.when(jnp.logical_and(s >= FINAL_LAG, s < total + FINAL_LAG))
            def _():
                activations(s - FINAL_LAG)

            @pl.when(jnp.logical_and(s >= chunks + FINAL_LAG, s < total + FINAL_LAG))
            def _():
                hx_copy(s - FINAL_LAG).start()

            @pl.when(jnp.logical_and(s >= total, s < total + chunks))
            def _():
                hx_copy(s - total).start()

            @pl.when(jnp.logical_and(s >= chunks + FORWARD_LAG, s < chunks + FORWARD_LAG + total))
            def _():
                i = (s - FORWARD_LAG) % total
                hx_copy(i).wait_recv()
                hf_copy(i).start()

            @pl.when(s >= chunks + BACK_LAG)
            def _():
                back((s - BACK_LAG) % total)

            return carry

        lax.fori_loop(0, total + chunks + BACK_LAG, step, 0)

        for group in range(GROUPS):
            for copy in cols_copies(group):
                copy.start()
        for group in (1, 2, 3):
            acc_copy(group).wait_recv()
        for kind in range(2):
            value = acc[0, kind] + acc_in[0, kind] + acc_in[1, kind] + acc_in[2, kind]
            tail[kind] = (cols[0, kind].astype(F32) + value).astype(BF16)
        for k in (2, 3, 1):
            for kind in range(2):
                tail_copy(kind, k).start()
        for kind in range(2):
            rows[kind, :, own] = tail[kind, mine]
        for k in (1, 2, 3):
            for kind in range(2):
                tail_copy(kind, k).wait_recv()
        row_copies = [pltpu.make_async_copy(rows.at[k], ref, row_sem.at[k]) for k, ref in enumerate((y_out, dx_out))]
        for copy in row_copies:
            copy.start()

        for k in (1, 2, 3):
            for kind in range(2):
                first_copy(kind, k).wait_send()
                tail_copy(kind, k).wait_send()
            spread_copy(k).wait_send()
            acc_copy(k).wait_send()

        def drain(i, carry):
            near_copy(i).wait_send()
            far_copy(i).wait_send()
            hc_copy(i).wait_send()
            hx_copy(i).wait_send()
            hf_copy(i).wait_send()
            for copy in out_copies(i):
                copy.wait()
            return carry

        lax.fori_loop(0, total, drain, 0)
        for group in range(GROUPS):
            for copy in cols_copies(group):
                copy.wait()
        for copy in row_copies:
            copy.wait()

    return kernel, total


def solution(mesh):
    row_spec = P(None, ("dp", "tp"), None)
    in_specs = (row_spec, P("dp", "tp"), P("dp", "tp"), P("tp", "dp"), row_spec)
    out_specs = (row_spec, row_spec, P("dp", "tp"), P("dp", "tp"), P("tp", "dp"))

    def local_step(x_loc, w_gate_loc, w_up_loc, w_down_loc, dy_loc):
        depth, hidden = w_gate_loc.shape
        micro, local_rows, model = x_loc.shape
        width = 512
        chunks = hidden // width
        kernel, total = make_kernel(chunks, width)
        dma = pltpu.SemaphoreType.DMA
        any_space = pl.BlockSpec(memory_space=pl.ANY)
        vmem = pl.BlockSpec(memory_space=pltpu.VMEM)
        hid_shape = jax.ShapeDtypeStruct((GROUPS, SLOTS, 16, hidden), BF16)
        col_shape = jax.ShapeDtypeStruct((GROUPS, SLOTS, 16, depth), BF16)
        row_shape = jax.ShapeDtypeStruct((16, model), BF16)
        outs = pl.pallas_call(
            kernel,
            out_shape=[row_shape, row_shape, hid_shape, hid_shape, hid_shape, col_shape, col_shape],
            in_specs=[vmem, vmem, any_space, any_space, any_space],
            out_specs=[any_space] * 7,
            scratch_shapes=[
                pltpu.VMEM((chunks, depth, width), BF16),
                pltpu.VMEM((chunks, depth, width), BF16),
                pltpu.VMEM((chunks, width, depth), BF16),
                pltpu.VMEM((GROUPS, 2, SLOTS, 16, depth), BF16),
                pltpu.VMEM((total, SLOTS, 3, 16, width), F32),
                pltpu.VMEM((total, 2, 3, 16, width), F32),
                pltpu.VMEM((total, 3, 16, width), F32),
                pltpu.VMEM((total, 3, SLOTS, 16, width), BF16),
                pltpu.VMEM((GROUPS, 2, SLOTS, 16, depth), F32),
                pltpu.VMEM((GROUPS - 1, 2, SLOTS, 16, depth), F32),
                pltpu.VMEM((2, SLOTS, 16, depth), BF16),
                pltpu.VMEM((2, 16, model), BF16),
                dma((chunks, 3)),
                dma((2, 3)), dma((2, 3)),
                dma((3,)), dma((3,)),
                dma((total,)), dma((total,)),
                dma((total,)), dma((total,)),
                dma((total,)), dma((total,)),
                dma((total,)), dma((total,)),
                dma((total,)), dma((total,)),
                dma((3,)), dma((3,)),
                dma((2, 3)), dma((2, 3)),
                dma((total, 3)), dma((GROUPS, 2)), dma((2,)),
            ],
            compiler_params=pltpu.CompilerParams(collective_id=0, has_side_effects=True, vmem_limit_bytes=67043328),
        )(x_loc.reshape(micro * local_rows, model), dy_loc.reshape(micro * local_rows, model), w_gate_loc, w_up_loc, w_down_loc)
        y_rows, dx_rows, h_all, da_all, db_all, x_cols, dy_cols = outs
        flat = lambda value: value.reshape(-1, value.shape[-1])
        over_rows = (((0,), (0,)), ((), ()))
        dw_gate = lax.dot_general(flat(x_cols), flat(da_all), over_rows, preferred_element_type=F32)
        dw_up = lax.dot_general(flat(x_cols), flat(db_all), over_rows, preferred_element_type=F32)
        dw_down = lax.dot_general(flat(h_all), flat(dy_cols), over_rows, preferred_element_type=F32)
        return y_rows.reshape(x_loc.shape), dx_rows.reshape(x_loc.shape), dw_gate, dw_up, dw_down

    return jax.shard_map(local_step, mesh=mesh, in_specs=in_specs, out_specs=out_specs, check_vma=False)
```

time: 500 us -> 149 us (0.30)
  waiting for transfers between devices: 201 us -> 0 us
  Pallas kernels: 0 us -> 122 us
  matrix products: 122 us -> 24.5 us
  blocking collectives: 92 us -> 0 us
  local copies, waits for them, and re-layouts: 33.8 us -> 1.33 us
  starting transfers between devices: 28 us -> 0 us
  between operations: 14 us -> 0.68 us
  other arithmetic: 7.55 us -> 0 us
    unnamed x10 -> x0, waiting for transfers between devices: 191 us -> none
    pallas_call x0 -> x1, Pallas kernels: none -> 122 us  [local_step(): pl.pallas_call(kernel, out_shape=[row_shape, row_shape, hid_shape, hid_sh...]
    dot_general x18 -> x3, matrix products: 122 us -> 24.5 us  [the longest x1 9.39 us: local_step(): lax.dot_general(flat(x_cols), flat(da_all), over_rows, preferred_element_...]
    all_gather x10 -> x0, blocking collectives: 92 us -> none  [the longest x4 36 us: token_columns(): gathered = lax.all_gather(spread, 'tp', axis=0)]
    unnamed x39 -> x14, local copies, waits for them, and re-layouts: 30.7 us -> 1.33 us
    all_to_all x8 -> x0, starting transfers between devices: 27.8 us -> none  [the longest x4 14.3 us: token_columns(): lax.all_to_all(rows_loc, 'dp', split_axis=1, concat_axis=0, tiled=True)]
    all_to_all x8 -> x0, waiting for transfers between devices: 10.3 us -> none  [the longest x4 7.98 us: to_rows(): lax.all_to_all(reduced, 'dp', split_axis=0, concat_axis=2, tiled=True)[0]]
    convert_element_type x4 -> x0, other arithmetic: 6.21 us -> none  [the longest x2 6.16 us: gate_grads(): return (grad_gate.astype(jnp.bfloat16), grad_up.astype(jnp.bfloat16))]
  transfers between devices with their start and end apart: 13 -> 0, of which waited for: 4 -> 0; matrix products, arithmetic and copies ran while one was open for 24% -> 0% of each run, Pallas kernels for 0% -> 0%
where the time goes in v1:
time: 149 us
  Pallas kernels  122 us (82%)
  matrix products  24.5 us (16%)
    pallas_call x1, Pallas kernels, local_step(): pl.pallas_call(kernel, out_shape=[row_shape, row_shape, hid_shape, hid_sh...  122 us
    dot_general x1, matrix products, local_step(): lax.dot_general(flat(x_cols), flat(da_all), over_rows, preferred_element_...  9.39 us
    dot_general x1, matrix products, local_step(): lax.dot_general(flat(x_cols), flat(db_all), over_rows, preferred_element_...  7.58 us
    dot_general x1, matrix products, local_step(): lax.dot_general(flat(h_all), flat(dy_cols), over_rows, preferred_element_...  7.57 us

profile of v1, /device:TPU:0, one launch (start us, length us, event | category | flops | bytes accessed | tf_op | source)
XLA Modules:
  0.0 148.6 jit_solution(1790331002117311879)
XLA Ops:
  0.6 122.0 %shard_map.92 = (bf16[16,4096]{1,0:T(8,128)(2,1)}, bf16[16,4096]{1,0:T(8,128)(2,1)}, bf16[4,4,16,3584]{3,2,1,0:T(8,128)(2,1)}, bf16[4,4,16,3584]{3,2,1,0:T(8,128...) custom-call(bf16[16,4096]{1,0:T(8,128)(2,1)} %bitcast.22, ...), custom_call_target="tpu_custom_call" | custom-call | tf_op jit(solution)/shard_map/pallas_call | solution.py:282
  122.7 0.0 copy-start.3
  122.7 0.0 copy-start.5
  122.7 9.4 %convolution_bitcast_fusion.2 = f32[1024,3584]{1,0:T(8,128)} fusion(bf16[4,4,16,1024]{3,2,1,0:T(8,128)(2,1)} %get-tuple-element.14, bf16[4,4,16,3584]{3,2,1,0:T(8,128)(2,1)} %get-tuple-element.15), kind=kOutput, calls=%fused_computation.2 | convolution fusion | flops 1879048192 | bytes 17039360 | tf_op jit(solution)/shard_map/dot_general | solution.py:317
  132.1 0.0 copy-done.3
  132.1 0.0 copy-done.5
  132.1 0.0 copy-start.2
  132.1 0.0 copy-start.4
  132.1 7.6 %convolution_bitcast_fusion.1 = f32[1024,3584]{1,0:T(8,128)} fusion(bf16[4,4,16,1024]{3,2,1,0:T(8,128)(2,1)S(1)} %copy-done.5, bf16[4,4,16,3584]{3,2,1,0:T(8,128)(2,1)S(1)} %copy-done.3), kind=kOutput, calls=%fused_computation.1 | convolution fusion | flops 1879048192 | bytes 17039360 | tf_op jit(solution)/shard_map/dot_general | solution.py:318
  139.7 0.0 copy-done.2
  139.7 0.0 copy-done.4
  139.7 0.0 copy-start.1
  139.7 0.0 copy-start
  139.7 7.6 %convolution_bitcast_fusion = f32[3584,1024]{1,0:T(8,128)} fusion(bf16[4,4,16,3584]{3,2,1,0:T(8,128)(2,1)S(1)} %copy-done.2, bf16[4,4,16,1024]{3,2,1,0:T(8,128)(2,1)S(1)} %copy-done.4), kind=kOutput, calls=%fused_computation | convolution fusion | flops 1879048192 | bytes 17039360 | tf_op jit(solution)/shard_map/dot_general | solution.py:319
  147.2 0.0 copy-done.1
  147.2 0.7 copy.15
  147.9 0.0 copy-done
  147.9 0.7 copy.16
Async XLA Ops:
  122.7 9.4 %copy-start.3 = (bf16[4,4,16,3584]{3,2,1,0:T(8,128)(2,1)S(1)}, bf16[4,4,16,3584]{3,2,1,0:T(8,128)(2,1)}, u32[]{:S(2)}) copy-start(bf16[4,4,16,3584]{3,2,1,0:T(8,128)(2,1)} %get-tuple-element.16) | copy-start | bytes 5505028
  122.7 9.4 %copy-start.5 = (bf16[4,4,16,1024]{3,2,1,0:T(8,128)(2,1)S(1)}, bf16[4,4,16,1024]{3,2,1,0:T(8,128)(2,1)}, u32[]{:S(2)}) copy-start(bf16[4,4,16,1024]{3,2,1,0:T(8,128)(2,1)} %get-tuple-element.14) | copy-start | bytes 1572868
  132.1 7.6 %copy-start.2 = (bf16[4,4,16,3584]{3,2,1,0:T(8,128)(2,1)S(1)}, bf16[4,4,16,3584]{3,2,1,0:T(8,128)(2,1)}, u32[]{:S(2)}) copy-start(bf16[4,4,16,3584]{3,2,1,0:T(8,128)(2,1)} %get-tuple-element.17) | copy-start | bytes 5505028
  132.1 7.6 %copy-start.4 = (bf16[4,4,16,1024]{3,2,1,0:T(8,128)(2,1)S(1)}, bf16[4,4,16,1024]{3,2,1,0:T(8,128)(2,1)}, u32[]{:S(2)}) copy-start(bf16[4,4,16,1024]{3,2,1,0:T(8,128)(2,1)} %get-tuple-element.18) | copy-start | bytes 1572868
  139.7 7.6 %copy-start.1 = (bf16[16,4096]{1,0:T(8,128)(2,1)S(1)}, bf16[16,4096]{1,0:T(8,128)(2,1)}, u32[]{:S(2)}) copy-start(bf16[16,4096]{1,0:T(8,128)(2,1)} %get-tuple-element.12) | copy-start | bytes 393220
  139.7 8.2 %copy-start = (bf16[16,4096]{1,0:T(8,128)(2,1)S(1)}, bf16[16,4096]{1,0:T(8,128)(2,1)}, u32[]{:S(2)}) copy-start(bf16[16,4096]{1,0:T(8,128)(2,1)} %get-tuple-element.13) | copy-start | bytes 393220

commit v2 on v1

--- a/solution.py
+++ b/solution.py
@@ -11,8 +11,9 @@
 GROUPS = 4
 SLOTS = 4
 FINAL_LAG = 4
-FORWARD_LAG = 7
-BACK_LAG = 8
+FORWARD_LAG = 12
+BACK_LAG = 13
+EARLY = 4
 
 
 def dot(lhs, rhs):
@@ -25,15 +26,14 @@
 
 def make_kernel(chunks, width):
     total = GROUPS * chunks
-    rest = total - chunks
-
-    def kernel(x_ref, dy_ref, wg_hbm, wu_hbm, wd_hbm,
+
+    def kernel(x_hbm, dy_hbm, wg_hbm, wu_hbm, wd_hbm,
                y_out, dx_out, h_out, da_out, db_out, xc_out, dyc_out,
-               wg, wu, wd, cols, part, near, far, hid, acc, acc_in, tail, rows,
+               wg, wu, wd, x_ref, dy_ref, cols, part, near, far, hid, acc, acc_in, tail, rows,
                w_sem, first_send, first_recv, spread_send, spread_recv,
                near_send, near_recv, far_send, far_recv,
                hc_send, hc_recv, hx_send, hx_recv, hf_send, hf_recv,
-               acc_send, acc_recv, tail_send, tail_recv, out_sem, cols_sem, row_sem):
+               acc_send, acc_recv, tail_send, tail_recv, out_sem, cols_sem, row_sem, in_sem):
         tp = lax.axis_index("tp")
         dp = lax.axis_index("dp")
         z, y = tp // 2, tp % 2
@@ -45,7 +45,10 @@
         depth = cols.shape[-1]
 
         def tp_peer(group):
-            return {"tp": ((z + group // 2) % 2) * 2 + (y + group % 2) % 2, "dp": dp}
+            return {"tp": ((z + group % 2) % 2) * 2 + (y + ((group + 1) // 2) % 2) % 2, "dp": dp}
+
+        def chunk_at(s):
+            return jnp.where(s < EARLY, s, jnp.where(s < total - chunks + EARLY, s + chunks - EARLY, s + chunks - total))
 
         def dp_peer(k):
             px, pc = (x + k // 2) % 2, (core + k % 2) % 2
@@ -105,6 +108,9 @@
             dst = rows.at[kind, :, pl.ds(pl.multiple_of(dp * depth, depth), depth)]
             return remote(tail.at[kind, slot], dst, tail_send.at[kind, k - 1], tail_recv.at[kind, k - 1], {"tp": tp, "dp": peer})
 
+        row_loads = [pltpu.make_async_copy(src, dst, in_sem.at[k]) for k, (src, dst) in enumerate(((x_hbm, x_ref), (dy_hbm, dy_ref)))]
+        for copy in row_loads:
+            copy.start()
         for c in range(chunks):
             for copy in weight_copies(c):
                 copy.start()
@@ -113,6 +119,8 @@
         for k in range(1, 4):
             pl.semaphore_signal(barrier, inc=1, device_id={"tp": tp, "dp": dp_peer(k)[0]}, device_id_type=MESH)
             pl.semaphore_signal(barrier, inc=1, device_id=tp_peer(k), device_id_type=MESH)
+        for copy in row_loads:
+            copy.wait()
         pl.semaphore_wait(barrier, 6)
 
         for k in (2, 3, 1):
@@ -131,7 +139,7 @@
         def products(i):
             group, c = i // chunks, i % chunks
 
-            @pl.when(group == 0)
+            @pl.when(group == jnp.where(c < EARLY, 0, 1))
             def _():
                 for copy in weight_copies(c):
                     copy.wait()
@@ -183,37 +191,37 @@
         def step(s, carry):
             @pl.when(s < total)
             def _():
-                products(s)
+                products(chunk_at(s))
 
             @pl.when(jnp.logical_and(s >= 1, s < total + 1))
             def _():
-                half_sum(s - 1)
+                half_sum(chunk_at(s - 1))
 
             @pl.when(jnp.logical_and(s >= FINAL_LAG, s < total + FINAL_LAG))
             def _():
-                activations(s - FINAL_LAG)
-
-            @pl.when(jnp.logical_and(s >= chunks + FINAL_LAG, s < total + FINAL_LAG))
-            def _():
-                hx_copy(s - FINAL_LAG).start()
+                activations(chunk_at(s - FINAL_LAG))
+
+            @pl.when(jnp.logical_and(s >= EARLY + FINAL_LAG, s < total - chunks + EARLY + FINAL_LAG))
+            def _():
+                hx_copy(s - FINAL_LAG + chunks - EARLY).start()
 
             @pl.when(jnp.logical_and(s >= total, s < total + chunks))
             def _():
                 hx_copy(s - total).start()
 
-            @pl.when(jnp.logical_and(s >= chunks + FORWARD_LAG, s < chunks + FORWARD_LAG + total))
-            def _():
-                i = (s - FORWARD_LAG) % total
+            @pl.when(jnp.logical_and(s >= FORWARD_LAG, s < FORWARD_LAG + total))
+            def _():
+                i = (s - FORWARD_LAG + chunks) % total
                 hx_copy(i).wait_recv()
                 hf_copy(i).start()
 
-            @pl.when(s >= chunks + BACK_LAG)
-            def _():
-                back((s - BACK_LAG) % total)
+            @pl.when(s >= BACK_LAG)
+            def _():
+                back((s - BACK_LAG + chunks) % total)
 
             return carry
 
-        lax.fori_loop(0, total + chunks + BACK_LAG, step, 0)
+        lax.fori_loop(0, total + BACK_LAG, step, 0)
 
         for group in range(GROUPS):
             for copy in cols_copies(group):
@@ -262,6 +270,85 @@
     return kernel, total
 
 
+def weight_grads(h, da, db, x_cols, dy_cols, width):
+    count, hidden = h.shape
+    depth = x_cols.shape[1]
+    chunks = hidden // width
+    ring = 4
+
+    def kernel(h_hbm, da_hbm, db_hbm, x_hbm, dy_hbm, dg_hbm, du_hbm, dd_hbm,
+               h_in, da_in, db_in, x_in, dy_in, x_t, g_tile, u_tile, d_tile, in_sem, row_sem, out_sem):
+        def span(c):
+            return pl.ds(pl.multiple_of(c * width, width), width)
+
+        def loads(c):
+            return [pltpu.make_async_copy(src.at[:, span(c)], dst.at[c], in_sem.at[k, c])
+                    for k, (src, dst) in enumerate(((da_hbm, da_in), (db_hbm, db_in), (h_hbm, h_in)))]
+
+        def stores(c):
+            slot = c % ring
+            return (pltpu.make_async_copy(g_tile.at[slot], dg_hbm.at[:, span(c)], out_sem.at[0, slot]),
+                    pltpu.make_async_copy(u_tile.at[slot], du_hbm.at[:, span(c)], out_sem.at[1, slot]),
+                    pltpu.make_async_copy(d_tile.at[slot], dd_hbm.at[span(c)], out_sem.at[2, slot]))
+
+        rows = [pltpu.make_async_copy(src, dst, row_sem.at[k]) for k, (src, dst) in enumerate(((x_hbm, x_in), (dy_hbm, dy_in)))]
+        rows[0].start()
+        for c in range(chunks):
+            for copy in loads(c):
+                copy.start()
+            if c == 0:
+                rows[1].start()
+        rows[0].wait()
+        x_t[...] = x_in[...].T
+        rows[1].wait()
+
+        def step(c, carry):
+            slot = c % ring
+            for k, value in enumerate(loads(c)):
+                value.wait()
+            old, new = stores(c - ring), stores(c)
+            for k in range(3):
+                @pl.when(c >= ring)
+                def _(k=k):
+                    old[k].wait()
+                if k == 0:
+                    g_tile[slot] = dot(x_t[...], da_in[c])
+                elif k == 1:
+                    u_tile[slot] = dot(x_t[...], db_in[c])
+                else:
+                    d_tile[slot] = dot(h_in[c].T, dy_in[...])
+                new[k].start()
+            return carry
+
+        lax.fori_loop(0, chunks, step, 0)
+        for c in range(chunks - ring, chunks):
+            for copy in stores(c):
+                copy.wait()
+
+    dma = pltpu.SemaphoreType.DMA
+    any_space = pl.BlockSpec(memory_space=pl.ANY)
+    return pl.pallas_call(
+        kernel,
+        out_shape=[jax.ShapeDtypeStruct((depth, hidden), F32), jax.ShapeDtypeStruct((depth, hidden), F32), jax.ShapeDtypeStruct((hidden, depth), F32)],
+        in_specs=[any_space] * 5,
+        out_specs=[any_space] * 3,
+        scratch_shapes=[
+            pltpu.VMEM((chunks, count, width), BF16),
+            pltpu.VMEM((chunks, count, width), BF16),
+            pltpu.VMEM((chunks, count, width), BF16),
+            pltpu.VMEM((count, depth), BF16),
+            pltpu.VMEM((count, depth), BF16),
+            pltpu.VMEM((depth, count), BF16),
+            pltpu.VMEM((ring, depth, width), F32),
+            pltpu.VMEM((ring, depth, width), F32),
+            pltpu.VMEM((ring, width, depth), F32),
+            dma((3, chunks)), dma((2,)), dma((3, ring)),
+        ],
+        compiler_params=pltpu.CompilerParams(vmem_limit_bytes=67043328),
+        cost_estimate=pl.CostEstimate(flops=6 * count * depth * hidden, bytes_accessed=12 * depth * hidden, transcendentals=0),
+    )(h, da, db, x_cols, dy_cols)
+
+
 def solution(mesh):
     row_spec = P(None, ("dp", "tp"), None)
     in_specs = (row_spec, P("dp", "tp"), P("dp", "tp"), P("tp", "dp"), row_spec)
@@ -275,19 +362,20 @@
         kernel, total = make_kernel(chunks, width)
         dma = pltpu.SemaphoreType.DMA
         any_space = pl.BlockSpec(memory_space=pl.ANY)
-        vmem = pl.BlockSpec(memory_space=pltpu.VMEM)
         hid_shape = jax.ShapeDtypeStruct((GROUPS, SLOTS, 16, hidden), BF16)
         col_shape = jax.ShapeDtypeStruct((GROUPS, SLOTS, 16, depth), BF16)
         row_shape = jax.ShapeDtypeStruct((16, model), BF16)
         outs = pl.pallas_call(
             kernel,
             out_shape=[row_shape, row_shape, hid_shape, hid_shape, hid_shape, col_shape, col_shape],
-            in_specs=[vmem, vmem, any_space, any_space, any_space],
+            in_specs=[any_space] * 5,
             out_specs=[any_space] * 7,
             scratch_shapes=[
                 pltpu.VMEM((chunks, depth, width), BF16),
                 pltpu.VMEM((chunks, depth, width), BF16),
                 pltpu.VMEM((chunks, width, depth), BF16),
+                pltpu.VMEM((16, model), BF16),
+                pltpu.VMEM((16, model), BF16),
                 pltpu.VMEM((GROUPS, 2, SLOTS, 16, depth), BF16),
                 pltpu.VMEM((total, SLOTS, 3, 16, width), F32),
                 pltpu.VMEM((total, 2, 3, 16, width), F32),
@@ -307,16 +395,13 @@
                 dma((total,)), dma((total,)),
                 dma((3,)), dma((3,)),
                 dma((2, 3)), dma((2, 3)),
-                dma((total, 3)), dma((GROUPS, 2)), dma((2,)),
+                dma((total, 3)), dma((GROUPS, 2)), dma((2,)), dma((2,)),
             ],
             compiler_params=pltpu.CompilerParams(collective_id=0, has_side_effects=True, vmem_limit_bytes=67043328),
         )(x_loc.reshape(micro * local_rows, model), dy_loc.reshape(micro * local_rows, model), w_gate_loc, w_up_loc, w_down_loc)
         y_rows, dx_rows, h_all, da_all, db_all, x_cols, dy_cols = outs
         flat = lambda value: value.reshape(-1, value.shape[-1])
-        over_rows = (((0,), (0,)), ((), ()))
-        dw_gate = lax.dot_general(flat(x_cols), flat(da_all), over_rows, preferred_element_type=F32)
-        dw_up = lax.dot_general(flat(x_cols), flat(db_all), over_rows, preferred_element_type=F32)
-        dw_down = lax.dot_general(flat(h_all), flat(dy_cols), over_rows, preferred_element_type=F32)
+        dw_gate, dw_up, dw_down = weight_grads(flat(h_all), flat(da_all), flat(db_all), flat(x_cols), flat(dy_cols), width)
         return y_rows.reshape(x_loc.shape), dx_rows.reshape(x_loc.shape), dw_gate, dw_up, dw_down
 
     return jax.shard_map(local_step, mesh=mesh, in_specs=in_specs, out_specs=out_specs, check_vma=False)

time: 149 us -> 145 us (0.973)
  matrix products: 24.5 us -> 0 us
  Pallas kernels: 122 us -> 141 us
  local copies, waits for them, and re-layouts: 1.33 us -> 3.14 us
    dot_general x3 -> x0, matrix products: 24.5 us -> none  [the longest x1 9.39 us: local_step(): lax.dot_general(flat(x_cols), flat(da_all), over_rows, preferred_element_...]
    pallas_call x0 -> x1, Pallas kernels: none -> 17.6 us  [weight_grads(): pl.pallas_call(kernel, out_shape=[jax.ShapeDtypeStruct((depth, hidden), F...]
    unnamed x14 -> x2, local copies, waits for them, and re-layouts: 1.33 us -> 3.14 us
    pallas_call x1, Pallas kernels: 122 us -> 124 us  [local_step(): pl.pallas_call(kernel, out_shape=[row_shape, row_shape, hid_shape, hid_sh...]
where the time goes in v2:
time: 145 us
  Pallas kernels  141 us (97%)
  local copies, waits for them, and re-layouts  3.14 us (2%)
    pallas_call x1, Pallas kernels, local_step(): pl.pallas_call(kernel, out_shape=[row_shape, row_shape, hid_shape, hid_sh...  124 us
    pallas_call x1, Pallas kernels, weight_grads(): pl.pallas_call(kernel, out_shape=[jax.ShapeDtypeStruct((depth, hidden), F...  17.6 us
    unnamed x2, local copies, waits for them, and re-layouts  3.14 us

profile of v2, /device:TPU:0, one launch (start us, length us, event | category | flops | bytes accessed | tf_op | source)
XLA Modules:
  0.0 144.9 jit_solution(12813668751004710879)
XLA Ops:
  0.6 123.5 %shard_map.92 = (bf16[16,4096]{1,0:T(8,128)(2,1)}, bf16[16,4096]{1,0:T(8,128)(2,1)}, bf16[4,4,16,3584]{3,2,1,0:T(8,128)(2,1)}, bf16[4,4,16,3584]{3,2,1,0:T(8,128...) custom-call(bf16[16,4096]{1,0:T(8,128)(2,1)} %bitcast.9, ...), custom_call_target="tpu_custom_call" | custom-call | tf_op jit(solution)/shard_map/pallas_call | solution.py:368
  124.2 17.6 %shard_map.93 = (f32[1024,3584]{1,0:T(8,128)}, f32[1024,3584]{1,0:T(8,128)}, f32[3584,1024]{1,0:T(8,128)}) custom-call(bf16[256,3584]{1,0:T(8,128)(2,1)} %bitcast.13, bf16[256,3584]{1,0:T(8,128)(2,1)} %bitcast.14, bf16[256,3584]{1,0:T(8,128)(2,1)} %bitcast.15, bf16[256,1024]{1,0:T(8,128)(2,1)} %bitcast.16, bf16[256,1024]{1,0:T(8,128)(2,1)} %bitcast.17), custom_call_target="tpu_custom_call" | custom-call | flops 5637144576 | bytes 44040192 | tf_op jit(solution)/shard_map/pallas_call | solution.py:330
  141.8 1.6 %copy.12 = bf16[2,8,4096]{2,1,0:T(8,128)(2,1)} copy(bf16[2,8,4096]{2,1,0:T(8,128)(2,1)} %bitcast.12) | data formatting | bytes 262144
  143.4 1.6 %copy.13 = bf16[2,8,4096]{2,1,0:T(8,128)(2,1)} copy(bf16[2,8,4096]{2,1,0:T(8,128)(2,1)} %bitcast.11) | data formatting | bytes 262144

commit v3 on v2

--- a/solution.py
+++ b/solution.py
@@ -28,12 +28,12 @@
     total = GROUPS * chunks
 
     def kernel(x_hbm, dy_hbm, wg_hbm, wu_hbm, wd_hbm,
-               y_out, dx_out, h_out, da_out, db_out, xc_out, dyc_out,
-               wg, wu, wd, x_ref, dy_ref, cols, part, near, far, hid, acc, acc_in, tail, rows,
+               rows, hid, cols, x_turned,
+               wg, wu, wd, x_ref, dy_ref, part, near, far, acc, acc_in, tail,
                w_sem, first_send, first_recv, spread_send, spread_recv,
                near_send, near_recv, far_send, far_recv,
                hc_send, hc_recv, hx_send, hx_recv, hf_send, hf_recv,
-               acc_send, acc_recv, tail_send, tail_recv, out_sem, cols_sem, row_sem, in_sem):
+               acc_send, acc_recv, tail_send, tail_recv, in_sem):
         tp = lax.axis_index("tp")
         dp = lax.axis_index("dp")
         z, y = tp // 2, tp % 2
@@ -45,7 +45,7 @@
         depth = cols.shape[-1]
 
         def tp_peer(group):
-            return {"tp": ((z + group % 2) % 2) * 2 + (y + ((group + 1) // 2) % 2) % 2, "dp": dp}
+            return {"tp": ((z + group // 2) % 2) * 2 + (y + group % 2) % 2, "dp": dp}
 
         def chunk_at(s):
             return jnp.where(s < EARLY, s, jnp.where(s < total - chunks + EARLY, s + chunks - EARLY, s + chunks - total))
@@ -92,16 +92,6 @@
 
         def acc_copy(group):
             return remote(acc.at[group], acc_in.at[group - 1], acc_send.at[group - 1], acc_recv.at[group - 1], tp_peer(group))
-
-        def out_copies(i):
-            group, c = i // chunks, i % chunks
-            span = pl.ds(pl.multiple_of(c * width, width), width)
-            return [pltpu.make_async_copy(hid.at[i, k], ref.at[group, :, :, span], out_sem.at[i, k])
-                    for k, ref in enumerate((h_out, da_out, db_out))]
-
-        def cols_copies(group):
-            return [pltpu.make_async_copy(cols.at[group, k], ref.at[group], cols_sem.at[group, k])
-                    for k, ref in enumerate((xc_out, dyc_out))]
 
         def tail_copy(kind, k):
             peer, slot = dp_peer(k)
@@ -176,8 +166,6 @@
             group, c = i // chunks, i % chunks
             hc_copy(i).wait_recv()
             hf_copy(i).wait_recv()
-            for copy in out_copies(i):
-                copy.start()
             h_rows = hid[i, 0].reshape(SLOTS * 16, width)
             da_rows = hid[i, 1].reshape(SLOTS * 16, width)
             db_rows = hid[i, 2].reshape(SLOTS * 16, width)
@@ -215,6 +203,10 @@
                 hx_copy(i).wait_recv()
                 hf_copy(i).start()
 
+            @pl.when(s == total + FINAL_LAG)
+            def _():
+                x_turned[...] = cols[:, 0].reshape(GROUPS * SLOTS * 16, depth).T
+
             @pl.when(s >= BACK_LAG)
             def _():
                 back((s - BACK_LAG + chunks) % total)
@@ -223,9 +215,6 @@
 
         lax.fori_loop(0, total + BACK_LAG, step, 0)
 
-        for group in range(GROUPS):
-            for copy in cols_copies(group):
-                copy.start()
         for group in (1, 2, 3):
             acc_copy(group).wait_recv()
         for kind in range(2):
@@ -239,10 +228,6 @@
         for k in (1, 2, 3):
             for kind in range(2):
                 tail_copy(kind, k).wait_recv()
-        row_copies = [pltpu.make_async_copy(rows.at[k], ref, row_sem.at[k]) for k, ref in enumerate((y_out, dx_out))]
-        for copy in row_copies:
-            copy.start()
-
         for k in (1, 2, 3):
             for kind in range(2):
                 first_copy(kind, k).wait_send()
@@ -256,97 +241,78 @@
             hc_copy(i).wait_send()
             hx_copy(i).wait_send()
             hf_copy(i).wait_send()
-            for copy in out_copies(i):
-                copy.wait()
             return carry
 
         lax.fori_loop(0, total, drain, 0)
-        for group in range(GROUPS):
-            for copy in cols_copies(group):
-                copy.wait()
-        for copy in row_copies:
-            copy.wait()
 
     return kernel, total
 
 
-def weight_grads(h, da, db, x_cols, dy_cols, width):
-    count, hidden = h.shape
-    depth = x_cols.shape[1]
-    chunks = hidden // width
+def finish(rows, hid, cols, x_turned):
+    _, local_rows, model = rows.shape
+    total, _, _, _, width = hid.shape
+    depth, count = x_turned.shape
+    chunks = total // GROUPS
+    hidden = chunks * width
     ring = 4
 
-    def kernel(h_hbm, da_hbm, db_hbm, x_hbm, dy_hbm, dg_hbm, du_hbm, dd_hbm,
-               h_in, da_in, db_in, x_in, dy_in, x_t, g_tile, u_tile, d_tile, in_sem, row_sem, out_sem):
-        def span(c):
-            return pl.ds(pl.multiple_of(c * width, width), width)
-
-        def loads(c):
-            return [pltpu.make_async_copy(src.at[:, span(c)], dst.at[c], in_sem.at[k, c])
-                    for k, (src, dst) in enumerate(((da_hbm, da_in), (db_hbm, db_in), (h_hbm, h_in)))]
+    def kernel(rows_ref, hid_ref, cols_ref, x_ref, y_hbm, dx_hbm, dg_hbm, du_hbm, dd_hbm, g_tile, u_tile, d_tile, row_sem, out_sem):
+        row_copies = [pltpu.make_async_copy(rows_ref.at[k], dst, row_sem.at[k]) for k, dst in enumerate((y_hbm, dx_hbm))]
+
+        def all_rows(c, k):
+            return jnp.concatenate([hid_ref[group * chunks + c, k].reshape(SLOTS * 16, width) for group in range(GROUPS)])
 
         def stores(c):
             slot = c % ring
-            return (pltpu.make_async_copy(g_tile.at[slot], dg_hbm.at[:, span(c)], out_sem.at[0, slot]),
-                    pltpu.make_async_copy(u_tile.at[slot], du_hbm.at[:, span(c)], out_sem.at[1, slot]),
-                    pltpu.make_async_copy(d_tile.at[slot], dd_hbm.at[span(c)], out_sem.at[2, slot]))
-
-        rows = [pltpu.make_async_copy(src, dst, row_sem.at[k]) for k, (src, dst) in enumerate(((x_hbm, x_in), (dy_hbm, dy_in)))]
-        rows[0].start()
-        for c in range(chunks):
-            for copy in loads(c):
-                copy.start()
-            if c == 0:
-                rows[1].start()
-        rows[0].wait()
-        x_t[...] = x_in[...].T
-        rows[1].wait()
+            span = pl.ds(pl.multiple_of(c * width, width), width)
+            return (pltpu.make_async_copy(g_tile.at[slot], dg_hbm.at[:, span], out_sem.at[0, slot]),
+                    pltpu.make_async_copy(u_tile.at[slot], du_hbm.at[:, span], out_sem.at[1, slot]),
+                    pltpu.make_async_copy(d_tile.at[slot], dd_hbm.at[span], out_sem.at[2, slot]))
 
         def step(c, carry):
             slot = c % ring
-            for k, value in enumerate(loads(c)):
-                value.wait()
             old, new = stores(c - ring), stores(c)
             for k in range(3):
                 @pl.when(c >= ring)
                 def _(k=k):
                     old[k].wait()
                 if k == 0:
-                    g_tile[slot] = dot(x_t[...], da_in[c])
+                    g_tile[slot] = dot(x_ref[...], all_rows(c, 1))
                 elif k == 1:
-                    u_tile[slot] = dot(x_t[...], db_in[c])
+                    u_tile[slot] = dot(x_ref[...], all_rows(c, 2))
                 else:
-                    d_tile[slot] = dot(h_in[c].T, dy_in[...])
+                    d_tile[slot] = dot(all_rows(c, 0).T, cols_ref[:, 1].reshape(count, depth))
                 new[k].start()
             return carry
 
         lax.fori_loop(0, chunks, step, 0)
+        for copy in row_copies:
+            copy.start()
         for c in range(chunks - ring, chunks):
             for copy in stores(c):
                 copy.wait()
+        for copy in row_copies:
+            copy.wait()
 
     dma = pltpu.SemaphoreType.DMA
     any_space = pl.BlockSpec(memory_space=pl.ANY)
+    vmem = pl.BlockSpec(memory_space=pltpu.VMEM)
+    row_shape = jax.ShapeDtypeStruct((local_rows, model), BF16)
+    held = [pltpu.with_memory_space_constraint(value, pltpu.VMEM) for value in (rows, hid, cols, x_turned)]
     return pl.pallas_call(
         kernel,
-        out_shape=[jax.ShapeDtypeStruct((depth, hidden), F32), jax.ShapeDtypeStruct((depth, hidden), F32), jax.ShapeDtypeStruct((hidden, depth), F32)],
-        in_specs=[any_space] * 5,
-        out_specs=[any_space] * 3,
+        out_shape=[row_shape, row_shape, jax.ShapeDtypeStruct((depth, hidden), F32), jax.ShapeDtypeStruct((depth, hidden), F32), jax.ShapeDtypeStruct((hidden, depth), F32)],
+        in_specs=[vmem] * 4,
+        out_specs=[any_space] * 5,
         scratch_shapes=[
-            pltpu.VMEM((chunks, count, width), BF16),
-            pltpu.VMEM((chunks, count, width), BF16),
-            pltpu.VMEM((chunks, count, width), BF16),
-            pltpu.VMEM((count, depth), BF16),
-            pltpu.VMEM((count, depth), BF16),
-            pltpu.VMEM((depth, count), BF16),
             pltpu.VMEM((ring, depth, width), F32),
             pltpu.VMEM((ring, depth, width), F32),
             pltpu.VMEM((ring, width, depth), F32),
-            dma((3, chunks)), dma((2,)), dma((3, ring)),
+            dma((2,)), dma((3, ring)),
         ],
-        compiler_params=pltpu.CompilerParams(vmem_limit_bytes=67043328),
+        compiler_params=pltpu.CompilerParams(vmem_limit_bytes=40 * 2**20),
         cost_estimate=pl.CostEstimate(flops=6 * count * depth * hidden, bytes_accessed=12 * depth * hidden, transcendentals=0),
-    )(h, da, db, x_cols, dy_cols)
+    )(*held)
 
 
 def solution(mesh):
@@ -362,29 +328,29 @@
         kernel, total = make_kernel(chunks, width)
         dma = pltpu.SemaphoreType.DMA
         any_space = pl.BlockSpec(memory_space=pl.ANY)
-        hid_shape = jax.ShapeDtypeStruct((GROUPS, SLOTS, 16, hidden), BF16)
-        col_shape = jax.ShapeDtypeStruct((GROUPS, SLOTS, 16, depth), BF16)
-        row_shape = jax.ShapeDtypeStruct((16, model), BF16)
+        vmem = pl.BlockSpec(memory_space=pltpu.VMEM)
         outs = pl.pallas_call(
             kernel,
-            out_shape=[row_shape, row_shape, hid_shape, hid_shape, hid_shape, col_shape, col_shape],
+            out_shape=[
+                pltpu.VMEM((2, micro * local_rows, model), BF16),
+                pltpu.VMEM((total, 3, SLOTS, 16, width), BF16),
+                pltpu.VMEM((GROUPS, 2, SLOTS, 16, depth), BF16),
+                pltpu.VMEM((depth, GROUPS * SLOTS * 16), BF16),
+            ],
             in_specs=[any_space] * 5,
-            out_specs=[any_space] * 7,
+            out_specs=[vmem] * 4,
             scratch_shapes=[
                 pltpu.VMEM((chunks, depth, width), BF16),
                 pltpu.VMEM((chunks, depth, width), BF16),
                 pltpu.VMEM((chunks, width, depth), BF16),
                 pltpu.VMEM((16, model), BF16),
                 pltpu.VMEM((16, model), BF16),
-                pltpu.VMEM((GROUPS, 2, SLOTS, 16, depth), BF16),
                 pltpu.VMEM((total, SLOTS, 3, 16, width), F32),
                 pltpu.VMEM((total, 2, 3, 16, width), F32),
                 pltpu.VMEM((total, 3, 16, width), F32),
-                pltpu.VMEM((total, 3, SLOTS, 16, width), BF16),
                 pltpu.VMEM((GROUPS, 2, SLOTS, 16, depth), F32),
                 pltpu.VMEM((GROUPS - 1, 2, SLOTS, 16, depth), F32),
                 pltpu.VMEM((2, SLOTS, 16, depth), BF16),
-                pltpu.VMEM((2, 16, model), BF16),
                 dma((chunks, 3)),
                 dma((2, 3)), dma((2, 3)),
                 dma((3,)), dma((3,)),
@@ -395,13 +361,11 @@
                 dma((total,)), dma((total,)),
                 dma((3,)), dma((3,)),
                 dma((2, 3)), dma((2, 3)),
-                dma((total, 3)), dma((GROUPS, 2)), dma((2,)), dma((2,)),
+                dma((2,)),
             ],
-            compiler_params=pltpu.CompilerParams(collective_id=0, has_side_effects=True, vmem_limit_bytes=67043328),
+            compiler_params=pltpu.CompilerParams(collective_id=0, has_side_effects=True, vmem_limit_bytes=53 * 2**20),
         )(x_loc.reshape(micro * local_rows, model), dy_loc.reshape(micro * local_rows, model), w_gate_loc, w_up_loc, w_down_loc)
-        y_rows, dx_rows, h_all, da_all, db_all, x_cols, dy_cols = outs
-        flat = lambda value: value.reshape(-1, value.shape[-1])
-        dw_gate, dw_up, dw_down = weight_grads(flat(h_all), flat(da_all), flat(db_all), flat(x_cols), flat(dy_cols), width)
+        y_rows, dx_rows, dw_gate, dw_up, dw_down = finish(*outs)
         return y_rows.reshape(x_loc.shape), dx_rows.reshape(x_loc.shape), dw_gate, dw_up, dw_down
 
     return jax.shard_map(local_step, mesh=mesh, in_specs=in_specs, out_specs=out_specs, check_vma=False)

time: 145 us -> 138 us (0.952)
  Pallas kernels: 141 us -> 137 us
  local copies, waits for them, and re-layouts: 3.14 us -> 0 us
    pallas_call x2, Pallas kernels: 141 us -> 137 us  [the longest x1 123 us: local_step(): pl.pallas_call(kernel, out_shape=[pltpu.VMEM((2, micro * local_rows, mode...]
    unnamed x2 -> x0, local copies, waits for them, and re-layouts: 3.14 us -> none
where the time goes in v3:
time: 138 us
  Pallas kernels  137 us (99%)
    pallas_call x1, Pallas kernels, local_step(): pl.pallas_call(kernel, out_shape=[pltpu.VMEM((2, micro * local_rows, mode...  123 us
    pallas_call x1, Pallas kernels, finish(): pl.pallas_call(kernel, out_shape=[row_shape, row_shape, jax.ShapeDtypeStr...  14.7 us

profile of v3, /device:TPU:0, one launch (start us, length us, event | category | flops | bytes accessed | tf_op | source)
XLA Modules:
  0.0 138.0 jit_solution(8937694669439377197)
XLA Ops:
  0.6 122.7 %shard_map.92 = (bf16[2,16,4096]{2,1,0:T(8,128)(2,1)S(1)}, bf16[28,3,4,16,512]{4,3,2,1,0:T(8,128)(2,1)S(1)}, bf16[4,2,4,16,1024]{4,3,2,1,0:T(8,128)(2,1)S(1)}, bf16[1024,256]{1,0:T(8,128)(2,1)S(1)}) custom-call(bf16[16,4096]{1,0:T(8,128)(2,1)} %bitcast.4, bf16[16,4096]{1,0:T(8,128)(2,1)} %bitcast.5, bf16[1024,3584]{1,0:T(8,128)(2,1)} %wg_hbm.1, ...), custom_call_target="tpu_custom_call" | custom-call | tf_op jit(solution)/shard_map/pallas_call | solution.py:332
  123.3 14.7 %shard_map.93 = (bf16[16,4096]{1,0:T(8,128)(2,1)}, bf16[16,4096]{1,0:T(8,128)(2,1)}, f32[1024,3584]{1,0:T(8,128)}, f32[1024,3584]{1,0:T(8,128)}, f32[3584,1024]{1,0:T(8,128)}) custom-call(bf16[2,16,4096]{2,1,0:T(8,128)(2,1)S(1)} %get-tuple-element.14.rows_ref, bf16[28,3,4,16,512]{4,3,2,1,0:T(8,128)(2,1)S(1)} %get-tuple-element.15.hid_ref, ...), custom_call_target="tpu_custom_call" | custom-call | flops 5637144576 | bytes 44040192 | tf_op jit(solution)/shard_map/pallas_call | solution.py:302

commit v4 on v3

--- a/solution.py
+++ b/solution.py
@@ -10,9 +10,9 @@
 BF16 = jnp.bfloat16
 GROUPS = 4
 SLOTS = 4
-FINAL_LAG = 4
-FORWARD_LAG = 12
-BACK_LAG = 13
+FINAL_LAG = 3
+FORWARD_LAG = 9
+BACK_LAG = 10
 EARLY = 4
 
 
@@ -33,7 +33,7 @@
                w_sem, first_send, first_recv, spread_send, spread_recv,
                near_send, near_recv, far_send, far_recv,
                hc_send, hc_recv, hx_send, hx_recv, hf_send, hf_recv,
-               acc_send, acc_recv, tail_send, tail_recv, in_sem):
+               acc_send, acc_recv, tail_send, tail_recv, in_sem, open_send, open_recv):
         tp = lax.axis_index("tp")
         dp = lax.axis_index("dp")
         z, y = tp // 2, tp % 2
@@ -75,6 +75,14 @@
         def near_copy(i):
             return remote(part.at[i, pl.ds(oc * 2, 2)], near.at[i], near_send.at[i], near_recv.at[i], core_peer)
 
+        def open_copy(k):
+            kinds = pl.ds(2 * k, 2 - k)
+            return remote(part.at[0, pl.ds(oc * 2, 2), kinds], near.at[0, :, kinds], open_send.at[k], open_recv.at[k], core_peer)
+
+        def open_far_copy(k):
+            kinds = pl.ds(2 * k, 2 - k)
+            return remote(near.at[0, ox, kinds], far.at[0, kinds], far_send.at[0], far_recv.at[0], x_peer)
+
         def far_copy(i):
             return remote(near.at[i, ox], far.at[i], far_send.at[i], far_recv.at[i], x_peer)
 
@@ -113,23 +121,35 @@
             copy.wait()
         pl.semaphore_wait(barrier, 6)
 
-        for k in (2, 3, 1):
-            for kind in range(2):
+        for kind in range(2):
+            for k in (2, 3, 1):
                 first_copy(kind, k).start()
         own = pl.ds(pl.multiple_of(dp * depth, depth), depth)
         cols[0, 0, mine] = x_ref[:, own]
         cols[0, 1, mine] = dy_ref[:, own]
         acc[...] = jnp.zeros_like(acc)
-        for k in (1, 2, 3):
-            for kind in range(2):
+        for copy in weight_copies(0):
+            copy.wait()
+        for kind in range(2):
+            for k in (1, 2, 3):
                 first_copy(kind, k).wait_recv()
-        for group in (1, 2, 3):
-            spread_copy(group).start()
+            rows_in = cols[0, kind].reshape(SLOTS * 16, depth)
+            for k in ((0, 1), (2,))[kind]:
+                value = dot_t(rows_in, wd[0]) if kind else dot(rows_in, (wg, wu)[k][0])
+                for slot in range(SLOTS):
+                    part[0, slot, k] = value[slot * 16:(slot + 1) * 16]
+            open_copy(kind).start()
+        spread_copy(1).start()
+        for k in range(2):
+            open_copy(k).wait_recv()
+            kinds = pl.ds(2 * k, 2 - k)
+            near[0, ox, kinds] = near[0, ox, kinds] + part[0, core * 2 + ox, kinds]
+            open_far_copy(k).start()
 
         def products(i):
             group, c = i // chunks, i % chunks
 
-            @pl.when(group == jnp.where(c < EARLY, 0, 1))
+            @pl.when(jnp.logical_and(i > 0, group == jnp.where(c < EARLY, 0, 1)))
             def _():
                 for copy in weight_copies(c):
                     copy.wait()
@@ -177,11 +197,23 @@
                 acc_copy(group).start()
 
         def step(s, carry):
+            @pl.when(s == EARLY)
+            def _():
+                half_sum(EARLY - 1)
+
             @pl.when(s < total)
             def _():
                 products(chunk_at(s))
 
-            @pl.when(jnp.logical_and(s >= 1, s < total + 1))
+            @pl.when(s == EARLY)
+            def _():
+                spread_copy(2).start()
+
+            @pl.when(s == EARLY + 3)
+            def _():
+                spread_copy(3).start()
+
+            @pl.when(jnp.logical_and(jnp.logical_and(s >= 2, s < total + 1), s != EARLY))
             def _():
                 half_sum(chunk_at(s - 1))
 
@@ -213,7 +245,7 @@
 
             return carry
 
-        lax.fori_loop(0, total + BACK_LAG, step, 0)
+        lax.fori_loop(1, total + BACK_LAG, step, 0)
 
         for group in (1, 2, 3):
             acc_copy(group).wait_recv()
@@ -235,8 +267,14 @@
             spread_copy(k).wait_send()
             acc_copy(k).wait_send()
 
+        for k in range(2):
+            open_copy(k).wait_send()
+
         def drain(i, carry):
-            near_copy(i).wait_send()
+            @pl.when(i > 0)
+            def _():
+                near_copy(i).wait_send()
+
             far_copy(i).wait_send()
             hc_copy(i).wait_send()
             hx_copy(i).wait_send()
@@ -361,7 +399,7 @@
                 dma((total,)), dma((total,)),
                 dma((3,)), dma((3,)),
                 dma((2, 3)), dma((2, 3)),
-                dma((2,)),
+                dma((2,)), dma((2,)), dma((2,)),
             ],
             compiler_params=pltpu.CompilerParams(collective_id=0, has_side_effects=True, vmem_limit_bytes=53 * 2**20),
         )(x_loc.reshape(micro * local_rows, model), dy_loc.reshape(micro * local_rows, model), w_gate_loc, w_up_loc, w_down_loc)

time: 138 us -> 137 us (level)
  no operation moved by 1% of the time
where the time goes in v4:
time: 137 us
  Pallas kernels  136 us (99%)
    pallas_call x1, Pallas kernels, local_step(): pl.pallas_call(kernel, out_shape=[pltpu.VMEM((2, micro * local_rows, mode...  122 us
    pallas_call x1, Pallas kernels, finish(): pl.pallas_call(kernel, out_shape=[row_shape, row_shape, jax.ShapeDtypeStr...  14.7 us

profile of v4, /device:TPU:0, one launch (start us, length us, event | category | flops | bytes accessed | tf_op | source)
XLA Modules:
  0.0 136.9 jit_solution(7895683786629891840)
XLA Ops:
  0.6 121.6 %shard_map.92 = (bf16[2,16,4096]{2,1,0:T(8,128)(2,1)S(1)}, bf16[28,3,4,16,512]{4,3,2,1,0:T(8,128)(2,1)S(1)}, bf16[4,2,4,16,1024]{4,3,2,1,0:T(8,128)(2,1)S(1)}, bf16[1024,256]{1,0:T(8,128)(2,1)S(1)}) custom-call(bf16[16,4096]{1,0:T(8,128)(2,1)} %bitcast.4, bf16[16,4096]{1,0:T(8,128)(2,1)} %bitcast.5, bf16[1024,3584]{1,0:T(8,128)(2,1)} %wg_hbm.1, ...), custom_call_target="tpu_custom_call" | custom-call | tf_op jit(solution)/shard_map/pallas_call | solution.py:370
  122.2 14.7 %shard_map.93 = (bf16[16,4096]{1,0:T(8,128)(2,1)}, bf16[16,4096]{1,0:T(8,128)(2,1)}, f32[1024,3584]{1,0:T(8,128)}, f32[1024,3584]{1,0:T(8,128)}, f32[3584,1024]{1,0:T(8,128)}) custom-call(bf16[2,16,4096]{2,1,0:T(8,128)(2,1)S(1)} %get-tuple-element.14.rows_ref, bf16[28,3,4,16,512]{4,3,2,1,0:T(8,128)(2,1)S(1)} %get-tuple-element.15.hid_ref, ...), custom_call_target="tpu_custom_call" | custom-call | flops 5637144576 | bytes 44040192 | tf_op jit(solution)/shard_map/pallas_call | solution.py:340

commit v5 on v4

--- a/solution.py
+++ b/solution.py
@@ -10,10 +10,10 @@
 BF16 = jnp.bfloat16
 GROUPS = 4
 SLOTS = 4
-FINAL_LAG = 3
-FORWARD_LAG = 9
-BACK_LAG = 10
-EARLY = 4
+FINAL_LAG = 4
+FORWARD_LAG = 10
+BACK_LAG = 11
+EARLY = 3
 
 
 def dot(lhs, rhs):
@@ -44,8 +44,8 @@
         mine = core * 2 + x
         depth = cols.shape[-1]
 
-        def tp_peer(group):
-            return {"tp": ((z + group // 2) % 2) * 2 + (y + group % 2) % 2, "dp": dp}
+        tp_peers = [{"tp": pz * 2 + py, "dp": dp} for pz, py in ((z, 1 - y), (1 - z, y), (1 - z, 1 - y))]
+        rows_of = (pl.ds(0, 8), pl.ds(8, 8))
 
         def chunk_at(s):
             return jnp.where(s < EARLY, s, jnp.where(s < total - chunks + EARLY, s + chunks - EARLY, s + chunks - total))
@@ -69,8 +69,11 @@
             src = (x_ref, dy_ref)[kind].at[:, pl.ds(pl.multiple_of(peer * depth, depth), depth)]
             return remote(src, cols.at[0, kind, mine], first_send.at[kind, k - 1], first_recv.at[kind, k - 1], {"tp": tp, "dp": peer})
 
-        def spread_copy(group):
-            return remote(cols.at[0], cols.at[group], spread_send.at[group - 1], spread_recv.at[group - 1], tp_peer(group))
+        def spread_copies(group, kind):
+            if group == 2:
+                return [remote(cols.at[0, kind], cols.at[2, kind], spread_send.at[1, kind, 0], spread_recv.at[1, kind, 0], tp_peers[2])]
+            return [remote(cols.at[0, kind, :, rows_of[group // 2]], cols.at[group, kind, :, rows_of[way]],
+                           spread_send.at[group - 1, kind, way], spread_recv.at[group - 1, kind, way], tp_peers[way]) for way in range(2)]
 
         def near_copy(i):
             return remote(part.at[i, pl.ds(oc * 2, 2)], near.at[i], near_send.at[i], near_recv.at[i], core_peer)
@@ -98,8 +101,11 @@
             there = hid.at[i, :, core * 2 + ox]
             return remote(there, there, hf_send.at[i], hf_recv.at[i], core_peer)
 
-        def acc_copy(group):
-            return remote(acc.at[group], acc_in.at[group - 1], acc_send.at[group - 1], acc_recv.at[group - 1], tp_peer(group))
+        def acc_copies(group):
+            if group == 2:
+                return [remote(acc.at[2], acc_in.at[2], acc_send.at[1, 0], acc_recv.at[1, 0], tp_peers[2])]
+            return [remote(acc.at[group, :, :, rows_of[way]], acc_in.at[way, :, :, rows_of[group // 2]],
+                           acc_send.at[group - 1, way], acc_recv.at[group - 1, way], tp_peers[way]) for way in range(2)]
 
         def tail_copy(kind, k):
             peer, slot = dp_peer(k)
@@ -116,7 +122,7 @@
         barrier = pltpu.get_barrier_semaphore()
         for k in range(1, 4):
             pl.semaphore_signal(barrier, inc=1, device_id={"tp": tp, "dp": dp_peer(k)[0]}, device_id_type=MESH)
-            pl.semaphore_signal(barrier, inc=1, device_id=tp_peer(k), device_id_type=MESH)
+            pl.semaphore_signal(barrier, inc=1, device_id=tp_peers[k - 1], device_id_type=MESH)
         for copy in row_loads:
             copy.wait()
         pl.semaphore_wait(barrier, 6)
@@ -133,13 +139,14 @@
         for kind in range(2):
             for k in (1, 2, 3):
                 first_copy(kind, k).wait_recv()
+            for copy in spread_copies(1, kind):
+                copy.start()
             rows_in = cols[0, kind].reshape(SLOTS * 16, depth)
             for k in ((0, 1), (2,))[kind]:
                 value = dot_t(rows_in, wd[0]) if kind else dot(rows_in, (wg, wu)[k][0])
                 for slot in range(SLOTS):
                     part[0, slot, k] = value[slot * 16:(slot + 1) * 16]
             open_copy(kind).start()
-        spread_copy(1).start()
         for k in range(2):
             open_copy(k).wait_recv()
             kinds = pl.ds(2 * k, 2 - k)
@@ -154,9 +161,12 @@
                 for copy in weight_copies(c):
                     copy.wait()
 
-            @pl.when(jnp.logical_and(group > 0, c == 0))
-            def _():
-                spread_copy(group).wait_recv()
+            for other in (1, 2, 3):
+                @pl.when(i == other * chunks)
+                def _(other=other):
+                    for kind in range(2):
+                        for copy in spread_copies(other, kind):
+                            copy.wait_recv()
 
             x_rows = cols[group, 0].reshape(SLOTS * 16, depth)
             dy_rows = cols[group, 1].reshape(SLOTS * 16, depth)
@@ -192,9 +202,11 @@
             acc[group, 0] += dot(h_rows, wd[c]).reshape(SLOTS, 16, depth)
             acc[group, 1] += (dot_t(da_rows, wg[c]) + dot_t(db_rows, wu[c])).reshape(SLOTS, 16, depth)
 
-            @pl.when(jnp.logical_and(group > 0, c == chunks - 1))
-            def _():
-                acc_copy(group).start()
+            for other in (1, 2, 3):
+                @pl.when(i == other * chunks + chunks - 1)
+                def _(other=other):
+                    for copy in acc_copies(other):
+                        copy.start()
 
         def step(s, carry):
             @pl.when(s == EARLY)
@@ -205,13 +217,12 @@
             def _():
                 products(chunk_at(s))
 
-            @pl.when(s == EARLY)
-            def _():
-                spread_copy(2).start()
-
-            @pl.when(s == EARLY + 3)
-            def _():
-                spread_copy(3).start()
+            for other in (2, 3):
+                @pl.when(s == EARLY + 3 * (other - 2))
+                def _(other=other):
+                    for kind in range(2):
+                        for copy in spread_copies(other, kind):
+                            copy.start()
 
             @pl.when(jnp.logical_and(jnp.logical_and(s >= 2, s < total + 1), s != EARLY))
             def _():
@@ -225,9 +236,14 @@
             def _():
                 hx_copy(s - FINAL_LAG + chunks - EARLY).start()
 
-            @pl.when(jnp.logical_and(s >= total, s < total + chunks))
-            def _():
-                hx_copy(s - total).start()
+            @pl.when(s == total)
+            def _():
+                for c in range(EARLY):
+                    hx_copy(c).start()
+
+            @pl.when(jnp.logical_and(s >= total - chunks + EARLY + FINAL_LAG, s < total + FINAL_LAG))
+            def _():
+                hx_copy(s - FINAL_LAG + chunks - total).start()
 
             @pl.when(jnp.logical_and(s >= FORWARD_LAG, s < FORWARD_LAG + total))
             def _():
@@ -248,12 +264,12 @@
         lax.fori_loop(1, total + BACK_LAG, step, 0)
 
         for group in (1, 2, 3):
-            acc_copy(group).wait_recv()
+            for copy in acc_copies(group):
+                copy.wait_recv()
         for kind in range(2):
             value = acc[0, kind] + acc_in[0, kind] + acc_in[1, kind] + acc_in[2, kind]
             tail[kind] = (cols[0, kind].astype(F32) + value).astype(BF16)
-        for k in (2, 3, 1):
-            for kind in range(2):
+            for k in (2, 3, 1):
                 tail_copy(kind, k).start()
         for kind in range(2):
             rows[kind, :, own] = tail[kind, mine]
@@ -264,8 +280,8 @@
             for kind in range(2):
                 first_copy(kind, k).wait_send()
                 tail_copy(kind, k).wait_send()
-            spread_copy(k).wait_send()
-            acc_copy(k).wait_send()
+            for copy in spread_copies(k, 0) + spread_copies(k, 1) + acc_copies(k):
+                copy.wait_send()
 
         for k in range(2):
             open_copy(k).wait_send()
@@ -391,13 +407,13 @@
                 pltpu.VMEM((2, SLOTS, 16, depth), BF16),
                 dma((chunks, 3)),
                 dma((2, 3)), dma((2, 3)),
-                dma((3,)), dma((3,)),
+                dma((3, 2, 2)), dma((3, 2, 2)),
                 dma((total,)), dma((total,)),
                 dma((total,)), dma((total,)),
                 dma((total,)), dma((total,)),
                 dma((total,)), dma((total,)),
                 dma((total,)), dma((total,)),
-                dma((3,)), dma((3,)),
+                dma((3, 2)), dma((3, 2)),
                 dma((2, 3)), dma((2, 3)),
                 dma((2,)), dma((2,)), dma((2,)),
             ],

time: 137 us -> 132 us (0.964)
  Pallas kernels: 136 us -> 131 us
    pallas_call x1, Pallas kernels: 122 us -> 116 us  [local_step(): pl.pallas_call(kernel, out_shape=[pltpu.VMEM((2, micro * local_rows, mode...]
where the time goes in v5:
time: 132 us
  Pallas kernels  131 us (99%)
    pallas_call x1, Pallas kernels, local_step(): pl.pallas_call(kernel, out_shape=[pltpu.VMEM((2, micro * local_rows, mode...  116 us
    pallas_call x1, Pallas kernels, finish(): pl.pallas_call(kernel, out_shape=[row_shape, row_shape, jax.ShapeDtypeStr...  14.7 us

profile of v5, /device:TPU:0, one launch (start us, length us, event | category | flops | bytes accessed | tf_op | source)
XLA Modules:
  0.0 131.5 jit_solution(460137522304883237)
XLA Ops:
  0.6 116.2 %shard_map.92 = (bf16[2,16,4096]{2,1,0:T(8,128)(2,1)S(1)}, bf16[28,3,4,16,512]{4,3,2,1,0:T(8,128)(2,1)S(1)}, bf16[4,2,4,16,1024]{4,3,2,1,0:T(8,128)(2,1)S(1)}, bf16[1024,256]{1,0:T(8,128)(2,1)S(1)}) custom-call(bf16[16,4096]{1,0:T(8,128)(2,1)} %bitcast.4, bf16[16,4096]{1,0:T(8,128)(2,1)} %bitcast.5, bf16[1024,3584]{1,0:T(8,128)(2,1)} %wg_hbm.1, ...), custom_call_target="tpu_custom_call" | custom-call | tf_op jit(solution)/shard_map/pallas_call | solution.py:386
  116.8 14.7 %shard_map.93 = (bf16[16,4096]{1,0:T(8,128)(2,1)}, bf16[16,4096]{1,0:T(8,128)(2,1)}, f32[1024,3584]{1,0:T(8,128)}, f32[1024,3584]{1,0:T(8,128)}, f32[3584,1024]{1,0:T(8,128)}) custom-call(bf16[2,16,4096]{2,1,0:T(8,128)(2,1)S(1)} %get-tuple-element.14.rows_ref, bf16[28,3,4,16,512]{4,3,2,1,0:T(8,128)(2,1)S(1)} %get-tuple-element.15.hid_ref, ...), custom_call_target="tpu_custom_call" | custom-call | flops 5637144576 | bytes 44040192 | tf_op jit(solution)/shard_map/pallas_call | solution.py:356

commit v6 on v5

--- a/solution.py
+++ b/solution.py
@@ -11,9 +11,9 @@
 GROUPS = 4
 SLOTS = 4
 FINAL_LAG = 4
-FORWARD_LAG = 10
-BACK_LAG = 11
-EARLY = 3
+FORWARD_LAG = 11
+BACK_LAG = 12
+EARLY = 4
 
 
 def dot(lhs, rhs):
@@ -41,7 +41,8 @@
         ox, oc = 1 - x, 1 - core
         core_peer = {"tp": tp, "dp": x * 2 + oc}
         x_peer = {"tp": tp, "dp": ox * 2 + core}
-        mine = core * 2 + x
+        home = core * 2 + x
+        owned = core * 2 + ox
         depth = cols.shape[-1]
 
         tp_peers = [{"tp": pz * 2 + py, "dp": dp} for pz, py in ((z, 1 - y), (1 - z, y), (1 - z, 1 - y))]
@@ -67,7 +68,7 @@
         def first_copy(kind, k):
             peer, _ = dp_peer(k)
             src = (x_ref, dy_ref)[kind].at[:, pl.ds(pl.multiple_of(peer * depth, depth), depth)]
-            return remote(src, cols.at[0, kind, mine], first_send.at[kind, k - 1], first_recv.at[kind, k - 1], {"tp": tp, "dp": peer})
+            return remote(src, cols.at[0, kind, home], first_send.at[kind, k - 1], first_recv.at[kind, k - 1], {"tp": tp, "dp": peer})
 
         def spread_copies(group, kind):
             if group == 2:
@@ -78,27 +79,28 @@
         def near_copy(i):
             return remote(part.at[i, pl.ds(oc * 2, 2)], near.at[i], near_send.at[i], near_recv.at[i], core_peer)
 
-        def open_copy(k):
-            kinds = pl.ds(2 * k, 2 - k)
-            return remote(part.at[0, pl.ds(oc * 2, 2), kinds], near.at[0, :, kinds], open_send.at[k], open_recv.at[k], core_peer)
-
-        def open_far_copy(k):
-            kinds = pl.ds(2 * k, 2 - k)
-            return remote(near.at[0, ox, kinds], far.at[0, kinds], far_send.at[0], far_recv.at[0], x_peer)
+        def open_copy(i, side, send, recv):
+            return remote(part.at[i, oc * 2 + side], near.at[i, side], send.at[i], recv.at[i], core_peer)
+
+        def here_copy(i):
+            return open_copy(i, x, open_send, open_recv)
+
+        def there_copy(i):
+            return open_copy(i, ox, near_send, near_recv)
 
         def far_copy(i):
-            return remote(near.at[i, ox], far.at[i], far_send.at[i], far_recv.at[i], x_peer)
+            return remote(near.at[i, x], far.at[i], far_send.at[i], far_recv.at[i], x_peer)
 
         def hc_copy(i):
-            here = hid.at[i, :, mine]
+            here = hid.at[i, :, owned]
             return remote(here, here, hc_send.at[i], hc_recv.at[i], core_peer)
 
         def hx_copy(i):
-            here = hid.at[i, :, mine]
+            here = hid.at[i, :, owned]
             return remote(here, here, hx_send.at[i], hx_recv.at[i], x_peer)
 
         def hf_copy(i):
-            there = hid.at[i, :, core * 2 + ox]
+            there = hid.at[i, :, home]
             return remote(there, there, hf_send.at[i], hf_recv.at[i], core_peer)
 
         def acc_copies(group):
@@ -112,6 +114,10 @@
             dst = rows.at[kind, :, pl.ds(pl.multiple_of(dp * depth, depth), depth)]
             return remote(tail.at[kind, slot], dst, tail_send.at[kind, k - 1], tail_recv.at[kind, k - 1], {"tp": tp, "dp": peer})
 
+        barrier = pltpu.get_barrier_semaphore()
+        for k in range(1, 4):
+            pl.semaphore_signal(barrier, inc=1, device_id=tp_peers[k - 1], device_id_type=MESH)
+            pl.semaphore_signal(barrier, inc=1, device_id={"tp": tp, "dp": dp_peer(k)[0]}, device_id_type=MESH)
         row_loads = [pltpu.make_async_copy(src, dst, in_sem.at[k]) for k, (src, dst) in enumerate(((x_hbm, x_ref), (dy_hbm, dy_ref)))]
         for copy in row_loads:
             copy.start()
@@ -119,44 +125,63 @@
             for copy in weight_copies(c):
                 copy.start()
 
-        barrier = pltpu.get_barrier_semaphore()
-        for k in range(1, 4):
-            pl.semaphore_signal(barrier, inc=1, device_id={"tp": tp, "dp": dp_peer(k)[0]}, device_id_type=MESH)
-            pl.semaphore_signal(barrier, inc=1, device_id=tp_peers[k - 1], device_id_type=MESH)
         for copy in row_loads:
             copy.wait()
         pl.semaphore_wait(barrier, 6)
 
         for kind in range(2):
-            for k in (2, 3, 1):
+            for k in (1, 2, 3):
                 first_copy(kind, k).start()
         own = pl.ds(pl.multiple_of(dp * depth, depth), depth)
-        cols[0, 0, mine] = x_ref[:, own]
-        cols[0, 1, mine] = dy_ref[:, own]
+        cols[0, 0, home] = x_ref[:, own]
+        cols[0, 1, home] = dy_ref[:, own]
         acc[...] = jnp.zeros_like(acc)
-        for copy in weight_copies(0):
-            copy.wait()
-        for kind in range(2):
-            for k in (1, 2, 3):
+
+        def half_products(i, side):
+            rows_in = [jnp.concatenate([cols[0, kind, side], cols[0, kind, 2 + side]]) for kind in range(2)]
+            for k, value in enumerate((dot(rows_in[0], wg[i]), dot(rows_in[0], wu[i]), dot_t(rows_in[1], wd[i]))):
+                part[i, side, k] = value[:16]
+                part[i, 2 + side, k] = value[16:]
+
+        def half_sum(i, copy):
+            copy.wait_recv()
+            near[i, x] = near[i, x] + part[i, home]
+            far_copy(i).start()
+
+        for kind in range(2):
+            first_copy(kind, 1).wait_recv()
+
+        def open_here(i, carry):
+            for copy in weight_copies(i):
+                copy.wait()
+            half_products(i, x)
+            here_copy(i).start()
+
+            @pl.when(i > 0)
+            def _():
+                half_sum(i - 1, here_copy(i - 1))
+
+            return carry
+
+        lax.fori_loop(0, EARLY, open_here, 0)
+        for kind in range(2):
+            for k in (2, 3):
                 first_copy(kind, k).wait_recv()
             for copy in spread_copies(1, kind):
                 copy.start()
-            rows_in = cols[0, kind].reshape(SLOTS * 16, depth)
-            for k in ((0, 1), (2,))[kind]:
-                value = dot_t(rows_in, wd[0]) if kind else dot(rows_in, (wg, wu)[k][0])
-                for slot in range(SLOTS):
-                    part[0, slot, k] = value[slot * 16:(slot + 1) * 16]
-            open_copy(kind).start()
-        for k in range(2):
-            open_copy(k).wait_recv()
-            kinds = pl.ds(2 * k, 2 - k)
-            near[0, ox, kinds] = near[0, ox, kinds] + part[0, core * 2 + ox, kinds]
-            open_far_copy(k).start()
+        half_sum(EARLY - 1, here_copy(EARLY - 1))
+
+        def open_there(i, carry):
+            half_products(i, ox)
+            there_copy(i).start()
+            return carry
+
+        lax.fori_loop(0, EARLY, open_there, 0)
 
         def products(i):
             group, c = i // chunks, i % chunks
 
-            @pl.when(jnp.logical_and(i > 0, group == jnp.where(c < EARLY, 0, 1)))
+            @pl.when(jnp.logical_and(group == 1, c >= EARLY))
             def _():
                 for copy in weight_copies(c):
                     copy.wait()
@@ -175,33 +200,37 @@
                     part[i, slot, k] = value[slot * 16:(slot + 1) * 16]
             near_copy(i).start()
 
-        def half_sum(i):
-            near_copy(i).wait_recv()
-            near[i, ox] = near[i, ox] + part[i, core * 2 + ox]
-            far_copy(i).start()
-
         def activations(i):
+            @pl.when(i < EARLY)
+            def _():
+                there_copy(i).wait_recv()
+
             far_copy(i).wait_recv()
-            gate = part[i, mine, 0] + near[i, x, 0] + far[i, 0]
-            up = part[i, mine, 1] + near[i, x, 1] + far[i, 1]
-            grad = part[i, mine, 2] + near[i, x, 2] + far[i, 2]
+            gate = part[i, owned, 0] + near[i, ox, 0] + far[i, 0]
+            up = part[i, owned, 1] + near[i, ox, 1] + far[i, 1]
+            grad = part[i, owned, 2] + near[i, ox, 2] + far[i, 2]
             sig = jax.nn.sigmoid(gate)
             act = gate * sig
-            hid[i, 0, mine] = (act * up).astype(BF16)
-            hid[i, 1, mine] = (grad * up * sig * (1.0 + gate * (1.0 - sig))).astype(BF16)
-            hid[i, 2, mine] = (grad * act).astype(BF16)
+            hid[i, 0, owned] = (act * up).astype(BF16)
+            hid[i, 1, owned] = (grad * up * sig * (1.0 + gate * (1.0 - sig))).astype(BF16)
+            hid[i, 2, owned] = (grad * act).astype(BF16)
             hc_copy(i).start()
+
+        def back_rows(i, k):
+            return hid[i, k].reshape(SLOTS * 16, width)
+
+        def add_y(group, i, c):
+            acc[group, 0] += dot(back_rows(i, 0), wd[c]).reshape(SLOTS, 16, depth)
+
+        def add_dx(group, i, c):
+            acc[group, 1] += (dot_t(back_rows(i, 1), wg[c]) + dot_t(back_rows(i, 2), wu[c])).reshape(SLOTS, 16, depth)
 
         def back(i):
             group, c = i // chunks, i % chunks
             hc_copy(i).wait_recv()
             hf_copy(i).wait_recv()
-            h_rows = hid[i, 0].reshape(SLOTS * 16, width)
-            da_rows = hid[i, 1].reshape(SLOTS * 16, width)
-            db_rows = hid[i, 2].reshape(SLOTS * 16, width)
-            acc[group, 0] += dot(h_rows, wd[c]).reshape(SLOTS, 16, depth)
-            acc[group, 1] += (dot_t(da_rows, wg[c]) + dot_t(db_rows, wu[c])).reshape(SLOTS, 16, depth)
-
+            add_y(group, i, c)
+            add_dx(group, i, c)
             for other in (1, 2, 3):
                 @pl.when(i == other * chunks + chunks - 1)
                 def _(other=other):
@@ -209,10 +238,6 @@
                         copy.start()
 
         def step(s, carry):
-            @pl.when(s == EARLY)
-            def _():
-                half_sum(EARLY - 1)
-
             @pl.when(s < total)
             def _():
                 products(chunk_at(s))
@@ -224,9 +249,10 @@
                         for copy in spread_copies(other, kind):
                             copy.start()
 
-            @pl.when(jnp.logical_and(jnp.logical_and(s >= 2, s < total + 1), s != EARLY))
-            def _():
-                half_sum(chunk_at(s - 1))
+            @pl.when(jnp.logical_and(s > EARLY, s < total + 1))
+            def _():
+                i = chunk_at(s - 1)
+                half_sum(i, near_copy(i))
 
             @pl.when(jnp.logical_and(s >= FINAL_LAG, s < total + FINAL_LAG))
             def _():
@@ -261,33 +287,35 @@
 
             return carry
 
-        lax.fori_loop(1, total + BACK_LAG, step, 0)
-
-        for group in (1, 2, 3):
-            for copy in acc_copies(group):
-                copy.wait_recv()
-        for kind in range(2):
+        lax.fori_loop(EARLY, total + BACK_LAG - 1, step, 0)
+
+        last = chunks - 1
+        hc_copy(last).wait_recv()
+        hf_copy(last).wait_recv()
+        for kind in range(2):
+            (add_y, add_dx)[kind](0, last, last)
+            if kind == 0:
+                for group in (1, 2, 3):
+                    for copy in acc_copies(group):
+                        copy.wait_recv()
             value = acc[0, kind] + acc_in[0, kind] + acc_in[1, kind] + acc_in[2, kind]
             tail[kind] = (cols[0, kind].astype(F32) + value).astype(BF16)
             for k in (2, 3, 1):
                 tail_copy(kind, k).start()
         for kind in range(2):
-            rows[kind, :, own] = tail[kind, mine]
+            rows[kind, :, own] = tail[kind, home]
+
         for k in (1, 2, 3):
-            for kind in range(2):
-                tail_copy(kind, k).wait_recv()
-        for k in (1, 2, 3):
-            for kind in range(2):
-                first_copy(kind, k).wait_send()
-                tail_copy(kind, k).wait_send()
-            for copy in spread_copies(k, 0) + spread_copies(k, 1) + acc_copies(k):
+            for copy in [first_copy(0, k), first_copy(1, k)] + spread_copies(k, 0) + spread_copies(k, 1) + acc_copies(k):
                 copy.wait_send()
 
-        for k in range(2):
-            open_copy(k).wait_send()
-
         def drain(i, carry):
-            @pl.when(i > 0)
+            @pl.when(i < EARLY)
+            def _():
+                here_copy(i).wait_send()
+                there_copy(i).wait_send()
+
+            @pl.when(i >= EARLY)
             def _():
                 near_copy(i).wait_send()
 
@@ -298,6 +326,9 @@
             return carry
 
         lax.fori_loop(0, total, drain, 0)
+        for kind in range(2):
+            for k in (1, 2, 3):
+                tail_copy(kind, k).wait()
 
     return kernel, total
 
@@ -415,7 +446,7 @@
                 dma((total,)), dma((total,)),
                 dma((3, 2)), dma((3, 2)),
                 dma((2, 3)), dma((2, 3)),
-                dma((2,)), dma((2,)), dma((2,)),
+                dma((2,)), dma((EARLY,)), dma((EARLY,)),
             ],
             compiler_params=pltpu.CompilerParams(collective_id=0, has_side_effects=True, vmem_limit_bytes=53 * 2**20),
         )(x_loc.reshape(micro * local_rows, model), dy_loc.reshape(micro * local_rows, model), w_gate_loc, w_up_loc, w_down_loc)

time: 132 us -> 129 us (0.977)
  Pallas kernels: 131 us -> 128 us
    pallas_call x1, Pallas kernels: 116 us -> 113 us  [local_step(): pl.pallas_call(kernel, out_shape=[pltpu.VMEM((2, micro * local_rows, mode...]
where the time goes in v6:
time: 129 us
  Pallas kernels  128 us (99%)
    pallas_call x1, Pallas kernels, local_step(): pl.pallas_call(kernel, out_shape=[pltpu.VMEM((2, micro * local_rows, mode...  113 us
    pallas_call x1, Pallas kernels, finish(): pl.pallas_call(kernel, out_shape=[row_shape, row_shape, jax.ShapeDtypeStr...  14.7 us

profile of v6, /device:TPU:0, one launch (start us, length us, event | category | flops | bytes accessed | tf_op | source)
XLA Modules:
  0.0 128.7 jit_solution(5342068272954818016)
XLA Ops:
  0.6 113.4 %shard_map.92 = (bf16[2,16,4096]{2,1,0:T(8,128)(2,1)S(1)}, bf16[28,3,4,16,512]{4,3,2,1,0:T(8,128)(2,1)S(1)}, bf16[4,2,4,16,1024]{4,3,2,1,0:T(8,128)(2,1)S(1)}, bf16[1024,256]{1,0:T(8,128)(2,1)S(1)}) custom-call(bf16[16,4096]{1,0:T(8,128)(2,1)} %bitcast.4, bf16[16,4096]{1,0:T(8,128)(2,1)} %bitcast.5, bf16[1024,3584]{1,0:T(8,128)(2,1)} %wg_hbm.1, ...), custom_call_target="tpu_custom_call" | custom-call | tf_op jit(solution)/shard_map/pallas_call | solution.py:417
  114.0 14.7 %shard_map.93 = (bf16[16,4096]{1,0:T(8,128)(2,1)}, bf16[16,4096]{1,0:T(8,128)(2,1)}, f32[1024,3584]{1,0:T(8,128)}, f32[1024,3584]{1,0:T(8,128)}, f32[3584,1024]{1,0:T(8,128)}) custom-call(bf16[2,16,4096]{2,1,0:T(8,128)(2,1)S(1)} %get-tuple-element.14.rows_ref, bf16[28,3,4,16,512]{4,3,2,1,0:T(8,128)(2,1)S(1)} %get-tuple-element.15.hid_ref, ...), custom_call_target="tpu_custom_call" | custom-call | flops 5637144576 | bytes 44040192 | tf_op jit(solution)/shard_map/pallas_call | solution.py:387

commit v7 on v6

--- a/solution.py
+++ b/solution.py
@@ -103,16 +103,17 @@
             there = hid.at[i, :, home]
             return remote(there, there, hf_send.at[i], hf_recv.at[i], core_peer)
 
-        def acc_copies(group):
+        def acc_copies(group, kind):
             if group == 2:
-                return [remote(acc.at[2], acc_in.at[2], acc_send.at[1, 0], acc_recv.at[1, 0], tp_peers[2])]
-            return [remote(acc.at[group, :, :, rows_of[way]], acc_in.at[way, :, :, rows_of[group // 2]],
-                           acc_send.at[group - 1, way], acc_recv.at[group - 1, way], tp_peers[way]) for way in range(2)]
-
-        def tail_copy(kind, k):
+                return [remote(acc.at[2, kind], acc_in.at[2, kind], acc_send.at[1, kind, 0], acc_recv.at[1, kind, 0], tp_peers[2])]
+            return [remote(acc.at[group, kind, :, rows_of[way]], acc_in.at[way, kind, :, rows_of[group // 2]],
+                           acc_send.at[group - 1, kind, way], acc_recv.at[group - 1, kind, way], tp_peers[way]) for way in range(2)]
+
+        def tail_copy(micro, kind, k):
             peer, slot = dp_peer(k)
-            dst = rows.at[kind, :, pl.ds(pl.multiple_of(dp * depth, depth), depth)]
-            return remote(tail.at[kind, slot], dst, tail_send.at[kind, k - 1], tail_recv.at[kind, k - 1], {"tp": tp, "dp": peer})
+            dst = rows.at[kind, rows_of[micro], pl.ds(pl.multiple_of(dp * depth, depth), depth)]
+            return remote(tail.at[kind, slot, rows_of[micro]], dst, tail_send.at[micro, kind, k - 1], tail_recv.at[micro, kind, k - 1],
+                          {"tp": tp, "dp": peer})
 
         barrier = pltpu.get_barrier_semaphore()
         for k in range(1, 4):
@@ -229,13 +230,13 @@
             group, c = i // chunks, i % chunks
             hc_copy(i).wait_recv()
             hf_copy(i).wait_recv()
-            add_y(group, i, c)
-            add_dx(group, i, c)
-            for other in (1, 2, 3):
-                @pl.when(i == other * chunks + chunks - 1)
-                def _(other=other):
-                    for copy in acc_copies(other):
-                        copy.start()
+            for kind in range(2):
+                (add_y, add_dx)[kind](group, i, c)
+                for other in (1, 2, 3):
+                    @pl.when(i == other * chunks + chunks - 1)
+                    def _(kind=kind, other=other):
+                        for copy in acc_copies(other, kind):
+                            copy.start()
 
         def step(s, carry):
             @pl.when(s < total)
@@ -294,19 +295,24 @@
         hf_copy(last).wait_recv()
         for kind in range(2):
             (add_y, add_dx)[kind](0, last, last)
-            if kind == 0:
-                for group in (1, 2, 3):
-                    for copy in acc_copies(group):
+        for kind in range(2):
+            for copy in acc_copies(1, kind) + acc_copies(2, kind):
+                copy.wait_recv()
+        for micro in range(2):
+            half = slice(8 * micro, 8 * micro + 8)
+            for kind in range(2):
+                if micro == 1:
+                    for copy in acc_copies(3, kind):
                         copy.wait_recv()
-            value = acc[0, kind] + acc_in[0, kind] + acc_in[1, kind] + acc_in[2, kind]
-            tail[kind] = (cols[0, kind].astype(F32) + value).astype(BF16)
-            for k in (2, 3, 1):
-                tail_copy(kind, k).start()
+                value = acc[0, kind, :, half] + acc_in[0, kind, :, half] + acc_in[1, kind, :, half] + acc_in[2, kind, :, half]
+                tail[kind, :, half] = (cols[0, kind, :, half].astype(F32) + value).astype(BF16)
+                for k in (2, 3, 1):
+                    tail_copy(micro, kind, k).start()
         for kind in range(2):
             rows[kind, :, own] = tail[kind, home]
 
         for k in (1, 2, 3):
-            for copy in [first_copy(0, k), first_copy(1, k)] + spread_copies(k, 0) + spread_copies(k, 1) + acc_copies(k):
+            for copy in [first_copy(0, k), first_copy(1, k)] + spread_copies(k, 0) + spread_copies(k, 1) + acc_copies(k, 0) + acc_copies(k, 1):
                 copy.wait_send()
 
         def drain(i, carry):
@@ -326,9 +332,10 @@
             return carry
 
         lax.fori_loop(0, total, drain, 0)
-        for kind in range(2):
-            for k in (1, 2, 3):
-                tail_copy(kind, k).wait()
+        for micro in range(2):
+            for kind in range(2):
+                for k in (1, 2, 3):
+                    tail_copy(micro, kind, k).wait()
 
     return kernel, total
 
@@ -347,35 +354,45 @@
         def all_rows(c, k):
             return jnp.concatenate([hid_ref[group * chunks + c, k].reshape(SLOTS * 16, width) for group in range(GROUPS)])
 
-        def stores(c):
+        def stores(c, part):
             slot = c % ring
             span = pl.ds(pl.multiple_of(c * width, width), width)
-            return (pltpu.make_async_copy(g_tile.at[slot], dg_hbm.at[:, span], out_sem.at[0, slot]),
-                    pltpu.make_async_copy(u_tile.at[slot], du_hbm.at[:, span], out_sem.at[1, slot]),
-                    pltpu.make_async_copy(d_tile.at[slot], dd_hbm.at[span], out_sem.at[2, slot]))
+            deep = pl.ds(part * (depth // 2), depth // 2)
+            wide = pl.ds(part * (width // 2), width // 2)
+            down = pl.ds(pl.multiple_of(c * width + part * (width // 2), width // 2), width // 2)
+            return (pltpu.make_async_copy(g_tile.at[slot, deep], dg_hbm.at[deep, span], out_sem.at[0, slot, part]),
+                    pltpu.make_async_copy(u_tile.at[slot, deep], du_hbm.at[deep, span], out_sem.at[1, slot, part]),
+                    pltpu.make_async_copy(d_tile.at[slot, wide], dd_hbm.at[down], out_sem.at[2, slot, part]))
 
         def step(c, carry):
             slot = c % ring
-            old, new = stores(c - ring), stores(c)
             for k in range(3):
-                @pl.when(c >= ring)
-                def _(k=k):
-                    old[k].wait()
-                if k == 0:
-                    g_tile[slot] = dot(x_ref[...], all_rows(c, 1))
-                elif k == 1:
-                    u_tile[slot] = dot(x_ref[...], all_rows(c, 2))
-                else:
-                    d_tile[slot] = dot(all_rows(c, 0).T, cols_ref[:, 1].reshape(count, depth))
-                new[k].start()
+                value = all_rows(c, (1, 2, 0)[k])
+                for part in range(2):
+                    old, new = stores(c - ring, part)[k], stores(c, part)[k]
+
+                    @pl.when(c >= ring)
+                    def _(old=old):
+                        old.wait()
+
+                    deep = slice(part * (depth // 2), (part + 1) * (depth // 2))
+                    wide = slice(part * (width // 2), (part + 1) * (width // 2))
+                    if k == 0:
+                        g_tile[slot, deep] = dot(x_ref[deep], value)
+                    elif k == 1:
+                        u_tile[slot, deep] = dot(x_ref[deep], value)
+                    else:
+                        d_tile[slot, wide] = dot(value[:, wide].T, cols_ref[:, 1].reshape(count, depth))
+                    new.start()
             return carry
 
         lax.fori_loop(0, chunks, step, 0)
         for copy in row_copies:
             copy.start()
         for c in range(chunks - ring, chunks):
-            for copy in stores(c):
-                copy.wait()
+            for part in range(2):
+                for copy in stores(c, part):
+                    copy.wait()
         for copy in row_copies:
             copy.wait()
 
@@ -393,7 +410,7 @@
             pltpu.VMEM((ring, depth, width), F32),
             pltpu.VMEM((ring, depth, width), F32),
             pltpu.VMEM((ring, width, depth), F32),
-            dma((2,)), dma((3, ring)),
+            dma((2,)), dma((3, ring, 2)),
         ],
         compiler_params=pltpu.CompilerParams(vmem_limit_bytes=40 * 2**20),
         cost_estimate=pl.CostEstimate(flops=6 * count * depth * hidden, bytes_accessed=12 * depth * hidden, transcendentals=0),
@@ -444,8 +461,8 @@
                 dma((total,)), dma((total,)),
                 dma((total,)), dma((total,)),
                 dma((total,)), dma((total,)),
-                dma((3, 2)), dma((3, 2)),
-                dma((2, 3)), dma((2, 3)),
+                dma((3, 2, 2)), dma((3, 2, 2)),
+                dma((2, 2, 3)), dma((2, 2, 3)),
                 dma((2,)), dma((EARLY,)), dma((EARLY,)),
             ],
             compiler_params=pltpu.CompilerParams(collective_id=0, has_side_effects=True, vmem_limit_bytes=53 * 2**20),

time: 129 us -> 130 us (level)
  no operation moved by 1% of the time
where the time goes in v7:
time: 130 us
  Pallas kernels  129 us (99%)
    pallas_call x1, Pallas kernels, local_step(): pl.pallas_call(kernel, out_shape=[pltpu.VMEM((2, micro * local_rows, mode...  115 us
    pallas_call x1, Pallas kernels, finish(): pl.pallas_call(kernel, out_shape=[row_shape, row_shape, jax.ShapeDtypeStr...  14.6 us

profile of v7, /device:TPU:0, one launch (start us, length us, event | category | flops | bytes accessed | tf_op | source)
XLA Modules:
  0.0 129.9 jit_solution(1101551440681322875)
XLA Ops:
  0.6 114.7 %shard_map.92 = (bf16[2,16,4096]{2,1,0:T(8,128)(2,1)S(1)}, bf16[28,3,4,16,512]{4,3,2,1,0:T(8,128)(2,1)S(1)}, bf16[4,2,4,16,1024]{4,3,2,1,0:T(8,128)(2,1)S(1)}, bf16[1024,256]{1,0:T(8,128)(2,1)S(1)}) custom-call(bf16[16,4096]{1,0:T(8,128)(2,1)} %bitcast.4, bf16[16,4096]{1,0:T(8,128)(2,1)} %bitcast.5, bf16[1024,3584]{1,0:T(8,128)(2,1)} %wg_hbm.1, ...), custom_call_target="tpu_custom_call" | custom-call | tf_op jit(solution)/shard_map/pallas_call | solution.py:434
  115.3 14.6 %shard_map.93 = (bf16[16,4096]{1,0:T(8,128)(2,1)}, bf16[16,4096]{1,0:T(8,128)(2,1)}, f32[1024,3584]{1,0:T(8,128)}, f32[1024,3584]{1,0:T(8,128)}, f32[3584,1024]{1,0:T(8,128)}) custom-call(bf16[2,16,4096]{2,1,0:T(8,128)(2,1)S(1)} %get-tuple-element.14.rows_ref, bf16[28,3,4,16,512]{4,3,2,1,0:T(8,128)(2,1)S(1)} %get-tuple-element.15.hid_ref, ...), custom_call_target="tpu_custom_call" | custom-call | flops 5637144576 | bytes 44040192 | tf_op jit(solution)/shard_map/pallas_call | solution.py:404

commit v8 on v6

--- a/solution.py
+++ b/solution.py
@@ -33,7 +33,7 @@
                w_sem, first_send, first_recv, spread_send, spread_recv,
                near_send, near_recv, far_send, far_recv,
                hc_send, hc_recv, hx_send, hx_recv, hf_send, hf_recv,
-               acc_send, acc_recv, tail_send, tail_recv, in_sem, open_send, open_recv):
+               acc_send, acc_recv, tail_send, tail_recv, in_sem, open_send, open_recv, lead_send, lead_recv):
         tp = lax.axis_index("tp")
         dp = lax.axis_index("dp")
         z, y = tp // 2, tp % 2
@@ -65,16 +65,23 @@
             return pltpu.make_async_remote_copy(src_ref=src, dst_ref=dst, send_sem=send, recv_sem=recv,
                                                 device_id=device, device_id_type=MESH)
 
-        def first_copy(kind, k):
+        def first_copy(micro, kind, k):
             peer, _ = dp_peer(k)
-            src = (x_ref, dy_ref)[kind].at[:, pl.ds(pl.multiple_of(peer * depth, depth), depth)]
-            return remote(src, cols.at[0, kind, home], first_send.at[kind, k - 1], first_recv.at[kind, k - 1], {"tp": tp, "dp": peer})
+            src = (x_ref, dy_ref)[kind].at[rows_of[micro], pl.ds(pl.multiple_of(peer * depth, depth), depth)]
+            return remote(src, cols.at[0, kind, home, rows_of[micro]], first_send.at[micro, kind, k - 1], first_recv.at[micro, kind, k - 1],
+                          {"tp": tp, "dp": peer})
 
         def spread_copies(group, kind):
             if group == 2:
                 return [remote(cols.at[0, kind], cols.at[2, kind], spread_send.at[1, kind, 0], spread_recv.at[1, kind, 0], tp_peers[2])]
             return [remote(cols.at[0, kind, :, rows_of[group // 2]], cols.at[group, kind, :, rows_of[way]],
                            spread_send.at[group - 1, kind, way], spread_recv.at[group - 1, kind, way], tp_peers[way]) for way in range(2)]
+
+        def lead_copies(far_side, kind):
+            side = ox if far_side else x
+            return [remote(cols.at[0, kind, core_slot * 2 + side, rows_of[0]], cols.at[1, kind, core_slot * 2 + side, rows_of[way]],
+                           lead_send.at[far_side, kind, core_slot, way], lead_recv.at[far_side, kind, core_slot, way], tp_peers[way])
+                    for core_slot in range(2) for way in range(2)]
 
         def near_copy(i):
             return remote(part.at[i, pl.ds(oc * 2, 2)], near.at[i], near_send.at[i], near_recv.at[i], core_peer)
@@ -129,9 +136,10 @@
             copy.wait()
         pl.semaphore_wait(barrier, 6)
 
-        for kind in range(2):
-            for k in (1, 2, 3):
-                first_copy(kind, k).start()
+        for micro in range(2):
+            for kind in range(2):
+                for k in (1, 2, 3):
+                    first_copy(micro, kind, k).start()
         own = pl.ds(pl.multiple_of(dp * depth, depth), depth)
         cols[0, 0, home] = x_ref[:, own]
         cols[0, 1, home] = dy_ref[:, own]
@@ -148,8 +156,12 @@
             near[i, x] = near[i, x] + part[i, home]
             far_copy(i).start()
 
-        for kind in range(2):
-            first_copy(kind, 1).wait_recv()
+        for micro in range(2):
+            for kind in range(2):
+                first_copy(micro, kind, 1).wait_recv()
+        for kind in range(2):
+            for copy in lead_copies(0, kind):
+                copy.start()
 
         def open_here(i, carry):
             for copy in weight_copies(i):
@@ -166,10 +178,14 @@
         lax.fori_loop(0, EARLY, open_here, 0)
         for kind in range(2):
             for k in (2, 3):
-                first_copy(kind, k).wait_recv()
-            for copy in spread_copies(1, kind):
+                first_copy(0, kind, k).wait_recv()
+            for copy in lead_copies(1, kind):
                 copy.start()
         half_sum(EARLY - 1, here_copy(EARLY - 1))
+
+        for kind in range(2):
+            for k in (2, 3):
+                first_copy(1, kind, k).wait_recv()
 
         def open_there(i, carry):
             half_products(i, ox)
@@ -190,7 +206,7 @@
                 @pl.when(i == other * chunks)
                 def _(other=other):
                     for kind in range(2):
-                        for copy in spread_copies(other, kind):
+                        for copy in spread_copies(other, kind) if other > 1 else lead_copies(0, kind) + lead_copies(1, kind):
                             copy.wait_recv()
 
             x_rows = cols[group, 0].reshape(SLOTS * 16, depth)
@@ -277,7 +293,7 @@
                 hx_copy(i).wait_recv()
                 hf_copy(i).start()
 
-            @pl.when(s == total + FINAL_LAG)
+            @pl.when(s == total - chunks)
             def _():
                 x_turned[...] = cols[:, 0].reshape(GROUPS * SLOTS * 16, depth).T
 
@@ -306,7 +322,11 @@
             rows[kind, :, own] = tail[kind, home]
 
         for k in (1, 2, 3):
-            for copy in [first_copy(0, k), first_copy(1, k)] + spread_copies(k, 0) + spread_copies(k, 1) + acc_copies(k):
+            for kind in range(2):
+                spread = spread_copies(k, kind) if k > 1 else lead_copies(0, kind) + lead_copies(1, kind)
+                for copy in [first_copy(0, kind, k), first_copy(1, kind, k)] + spread:
+                    copy.wait_send()
+            for copy in acc_copies(k):
                 copy.wait_send()
 
         def drain(i, carry):
@@ -340,6 +360,7 @@
     chunks = total // GROUPS
     hidden = chunks * width
     ring = 4
+    high = 128
 
     def kernel(rows_ref, hid_ref, cols_ref, x_ref, y_hbm, dx_hbm, dg_hbm, du_hbm, dd_hbm, g_tile, u_tile, d_tile, row_sem, out_sem):
         row_copies = [pltpu.make_async_copy(rows_ref.at[k], dst, row_sem.at[k]) for k, dst in enumerate((y_hbm, dx_hbm))]
@@ -347,35 +368,42 @@
         def all_rows(c, k):
             return jnp.concatenate([hid_ref[group * chunks + c, k].reshape(SLOTS * 16, width) for group in range(GROUPS)])
 
-        def stores(c):
-            slot = c % ring
+        def block(k, b):
+            span = pl.ds(pl.multiple_of(b * high, high), high)
+            return pltpu.make_async_copy((g_tile, u_tile)[k].at[b % ring], (dg_hbm, du_hbm)[k].at[span], out_sem.at[k, b % ring])
+
+        def tile(c):
             span = pl.ds(pl.multiple_of(c * width, width), width)
-            return (pltpu.make_async_copy(g_tile.at[slot], dg_hbm.at[:, span], out_sem.at[0, slot]),
-                    pltpu.make_async_copy(u_tile.at[slot], du_hbm.at[:, span], out_sem.at[1, slot]),
-                    pltpu.make_async_copy(d_tile.at[slot], dd_hbm.at[span], out_sem.at[2, slot]))
-
-        def step(c, carry):
-            slot = c % ring
-            old, new = stores(c - ring), stores(c)
-            for k in range(3):
-                @pl.when(c >= ring)
+            return pltpu.make_async_copy(d_tile.at[c % ring], dd_hbm.at[span], out_sem.at[2, c % ring])
+
+        def across(b, carry):
+            x_block = x_ref[pl.ds(pl.multiple_of(b * high, high), high)]
+            for k, held in enumerate((g_tile, u_tile)):
+                @pl.when(b >= ring)
                 def _(k=k):
-                    old[k].wait()
-                if k == 0:
-                    g_tile[slot] = dot(x_ref[...], all_rows(c, 1))
-                elif k == 1:
-                    u_tile[slot] = dot(x_ref[...], all_rows(c, 2))
-                else:
-                    d_tile[slot] = dot(all_rows(c, 0).T, cols_ref[:, 1].reshape(count, depth))
-                new[k].start()
-            return carry
-
-        lax.fori_loop(0, chunks, step, 0)
+                    block(k, b - ring).wait()
+                for c in range(chunks):
+                    held[b % ring, :, c * width:(c + 1) * width] = dot(x_block, all_rows(c, k + 1))
+                block(k, b).start()
+            return carry
+
+        def down(c, carry):
+            @pl.when(c >= ring)
+            def _():
+                tile(c - ring).wait()
+            d_tile[c % ring] = dot(all_rows(c, 0).T, cols_ref[:, 1].reshape(count, depth))
+            tile(c).start()
+            return carry
+
+        lax.fori_loop(0, depth // high, across, 0)
         for copy in row_copies:
             copy.start()
+        lax.fori_loop(0, chunks, down, 0)
+        for b in range(depth // high - ring, depth // high):
+            for k in range(2):
+                block(k, b).wait()
         for c in range(chunks - ring, chunks):
-            for copy in stores(c):
-                copy.wait()
+            tile(c).wait()
         for copy in row_copies:
             copy.wait()
 
@@ -390,8 +418,8 @@
         in_specs=[vmem] * 4,
         out_specs=[any_space] * 5,
         scratch_shapes=[
-            pltpu.VMEM((ring, depth, width), F32),
-            pltpu.VMEM((ring, depth, width), F32),
+            pltpu.VMEM((ring, high, hidden), F32),
+            pltpu.VMEM((ring, high, hidden), F32),
             pltpu.VMEM((ring, width, depth), F32),
             dma((2,)), dma((3, ring)),
         ],
@@ -437,7 +465,7 @@
                 pltpu.VMEM((GROUPS - 1, 2, SLOTS, 16, depth), F32),
                 pltpu.VMEM((2, SLOTS, 16, depth), BF16),
                 dma((chunks, 3)),
-                dma((2, 3)), dma((2, 3)),
+                dma((2, 2, 3)), dma((2, 2, 3)),
                 dma((3, 2, 2)), dma((3, 2, 2)),
                 dma((total,)), dma((total,)),
                 dma((total,)), dma((total,)),
@@ -447,6 +475,7 @@
                 dma((3, 2)), dma((3, 2)),
                 dma((2, 3)), dma((2, 3)),
                 dma((2,)), dma((EARLY,)), dma((EARLY,)),
+                dma((2, 2, 2, 2)), dma((2, 2, 2, 2)),
             ],
             compiler_params=pltpu.CompilerParams(collective_id=0, has_side_effects=True, vmem_limit_bytes=53 * 2**20),
         )(x_loc.reshape(micro * local_rows, model), dy_loc.reshape(micro * local_rows, model), w_gate_loc, w_up_loc, w_down_loc)

time: 129 us -> 128 us (level)
  no operation moved by 1% of the time
where the time goes in v8:
time: 128 us
  Pallas kernels  128 us (100%)
    pallas_call x1, Pallas kernels, local_step(): pl.pallas_call(kernel, out_shape=[pltpu.VMEM((2, micro * local_rows, mode...  113 us
    pallas_call x1, Pallas kernels, finish(): pl.pallas_call(kernel, out_shape=[row_shape, row_shape, jax.ShapeDtypeStr...  14.7 us

profile of v8, /device:TPU:0, one launch (start us, length us, event | category | flops | bytes accessed | tf_op | source)
XLA Modules:
  0.0 128.3 jit_solution(6710375501891943682)
XLA Ops:
  0.6 113.0 %shard_map.92 = (bf16[2,16,4096]{2,1,0:T(8,128)(2,1)S(1)}, bf16[28,3,4,16,512]{4,3,2,1,0:T(8,128)(2,1)S(1)}, bf16[4,2,4,16,1024]{4,3,2,1,0:T(8,128)(2,1)S(1)}, bf16[1024,256]{1,0:T(8,128)(2,1)S(1)}) custom-call(bf16[16,4096]{1,0:T(8,128)(2,1)} %bitcast.4, bf16[16,4096]{1,0:T(8,128)(2,1)} %bitcast.5, bf16[1024,3584]{1,0:T(8,128)(2,1)} %wg_hbm.1, ...), custom_call_target="tpu_custom_call" | custom-call | tf_op jit(solution)/shard_map/pallas_call | solution.py:445
  113.6 14.7 %shard_map.93 = (bf16[16,4096]{1,0:T(8,128)(2,1)}, bf16[16,4096]{1,0:T(8,128)(2,1)}, f32[1024,3584]{1,0:T(8,128)}, f32[1024,3584]{1,0:T(8,128)}, f32[3584,1024]{1,0:T(8,128)}) custom-call(bf16[2,16,4096]{2,1,0:T(8,128)(2,1)S(1)} %get-tuple-element.14.rows_ref, bf16[28,3,4,16,512]{4,3,2,1,0:T(8,128)(2,1)S(1)} %get-tuple-element.15.hid_ref, ...), custom_call_target="tpu_custom_call" | custom-call | flops 5637144576 | bytes 44040192 | tf_op jit(solution)/shard_map/pallas_call | solution.py:415

commit v9 on v8

--- a/solution.py
+++ b/solution.py
@@ -11,8 +11,8 @@
 GROUPS = 4
 SLOTS = 4
 FINAL_LAG = 4
-FORWARD_LAG = 11
-BACK_LAG = 12
+FORWARD_LAG = 10
+BACK_LAG = 11
 EARLY = 4
 
 

time: 128 us -> 128 us (level)
  no operation moved by 1% of the time
where the time goes in v9:
time: 128 us
  Pallas kernels  128 us (100%)
    pallas_call x1, Pallas kernels, local_step(): pl.pallas_call(kernel, out_shape=[pltpu.VMEM((2, micro * local_rows, mode...  113 us
    pallas_call x1, Pallas kernels, finish(): pl.pallas_call(kernel, out_shape=[row_shape, row_shape, jax.ShapeDtypeStr...  14.7 us

profile of v9, /device:TPU:0, one launch (start us, length us, event | category | flops | bytes accessed | tf_op | source)
XLA Modules:
  0.0 128.3 jit_solution(17378871861346726821)
XLA Ops:
  0.6 113.0 %shard_map.92 = (bf16[2,16,4096]{2,1,0:T(8,128)(2,1)S(1)}, bf16[28,3,4,16,512]{4,3,2,1,0:T(8,128)(2,1)S(1)}, bf16[4,2,4,16,1024]{4,3,2,1,0:T(8,128)(2,1)S(1)}, bf16[1024,256]{1,0:T(8,128)(2,1)S(1)}) custom-call(bf16[16,4096]{1,0:T(8,128)(2,1)} %bitcast.4, bf16[16,4096]{1,0:T(8,128)(2,1)} %bitcast.5, bf16[1024,3584]{1,0:T(8,128)(2,1)} %wg_hbm.1, ...), custom_call_target="tpu_custom_call" | custom-call | tf_op jit(solution)/shard_map/pallas_call | solution.py:445
  113.6 14.7 %shard_map.93 = (bf16[16,4096]{1,0:T(8,128)(2,1)}, bf16[16,4096]{1,0:T(8,128)(2,1)}, f32[1024,3584]{1,0:T(8,128)}, f32[1024,3584]{1,0:T(8,128)}, f32[3584,1024]{1,0:T(8,128)}) custom-call(bf16[2,16,4096]{2,1,0:T(8,128)(2,1)S(1)} %get-tuple-element.14.rows_ref, bf16[28,3,4,16,512]{4,3,2,1,0:T(8,128)(2,1)S(1)} %get-tuple-element.15.hid_ref, ...), custom_call_target="tpu_custom_call" | custom-call | flops 5637144576 | bytes 44040192 | tf_op jit(solution)/shard_map/pallas_call | solution.py:415

commit v10 on v9

--- a/solution.py
+++ b/solution.py
@@ -33,7 +33,7 @@
                w_sem, first_send, first_recv, spread_send, spread_recv,
                near_send, near_recv, far_send, far_recv,
                hc_send, hc_recv, hx_send, hx_recv, hf_send, hf_recv,
-               acc_send, acc_recv, tail_send, tail_recv, in_sem, open_send, open_recv, lead_send, lead_recv):
+               acc_send, acc_recv, tail_send, tail_recv, in_sem, open_recv, lead_send, lead_recv):
         tp = lax.axis_index("tp")
         dp = lax.axis_index("dp")
         z, y = tp // 2, tp % 2
@@ -48,6 +48,12 @@
         tp_peers = [{"tp": pz * 2 + py, "dp": dp} for pz, py in ((z, 1 - y), (1 - z, y), (1 - z, 1 - y))]
         rows_of = (pl.ds(0, 8), pl.ds(8, 8))
 
+        def place(i):
+            return jnp.where(i < EARLY, i, jnp.where(i < chunks, i + total - chunks, i - chunks + EARLY))
+
+        def turn(i):
+            return (i + total - chunks) % total
+
         def chunk_at(s):
             return jnp.where(s < EARLY, s, jnp.where(s < total - chunks + EARLY, s + chunks - EARLY, s + chunks - total))
 
@@ -68,58 +74,58 @@
         def first_copy(micro, kind, k):
             peer, _ = dp_peer(k)
             src = (x_ref, dy_ref)[kind].at[rows_of[micro], pl.ds(pl.multiple_of(peer * depth, depth), depth)]
-            return remote(src, cols.at[0, kind, home, rows_of[micro]], first_send.at[micro, kind, k - 1], first_recv.at[micro, kind, k - 1],
+            return remote(src, cols.at[0, kind, home, rows_of[micro]], first_send.at[0], first_recv.at[0 if k == 1 else 1 + micro],
                           {"tp": tp, "dp": peer})
 
         def spread_copies(group, kind):
             if group == 2:
-                return [remote(cols.at[0, kind], cols.at[2, kind], spread_send.at[1, kind, 0], spread_recv.at[1, kind, 0], tp_peers[2])]
+                return [remote(cols.at[0, kind], cols.at[2, kind], spread_send.at[0], spread_recv.at[0], tp_peers[2])]
             return [remote(cols.at[0, kind, :, rows_of[group // 2]], cols.at[group, kind, :, rows_of[way]],
-                           spread_send.at[group - 1, kind, way], spread_recv.at[group - 1, kind, way], tp_peers[way]) for way in range(2)]
+                           spread_send.at[0], spread_recv.at[1], tp_peers[way]) for way in range(2)]
 
         def lead_copies(far_side, kind):
             side = ox if far_side else x
             return [remote(cols.at[0, kind, core_slot * 2 + side, rows_of[0]], cols.at[1, kind, core_slot * 2 + side, rows_of[way]],
-                           lead_send.at[far_side, kind, core_slot, way], lead_recv.at[far_side, kind, core_slot, way], tp_peers[way])
+                           lead_send.at[0], lead_recv.at[0], tp_peers[way])
                     for core_slot in range(2) for way in range(2)]
 
         def near_copy(i):
-            return remote(part.at[i, pl.ds(oc * 2, 2)], near.at[i], near_send.at[i], near_recv.at[i], core_peer)
-
-        def open_copy(i, side, send, recv):
-            return remote(part.at[i, oc * 2 + side], near.at[i, side], send.at[i], recv.at[i], core_peer)
+            return remote(part.at[i, pl.ds(oc * 2, 2)], near.at[i], near_send.at[0], near_recv.at[place(i) % 8], core_peer)
+
+        def open_copy(i, side, recv):
+            return remote(part.at[i, oc * 2 + side], near.at[i, side], near_send.at[0], recv, core_peer)
 
         def here_copy(i):
-            return open_copy(i, x, open_send, open_recv)
+            return open_copy(i, x, open_recv.at[i])
 
         def there_copy(i):
-            return open_copy(i, ox, near_send, near_recv)
+            return open_copy(i, ox, near_recv.at[i % 8])
 
         def far_copy(i):
-            return remote(near.at[i, x], far.at[i], far_send.at[i], far_recv.at[i], x_peer)
+            return remote(near.at[i, x], far.at[i], far_send.at[0], far_recv.at[place(i) % 10], x_peer)
 
         def hc_copy(i):
             here = hid.at[i, :, owned]
-            return remote(here, here, hc_send.at[i], hc_recv.at[i], core_peer)
+            return remote(here, here, hc_send.at[0], hc_recv.at[jnp.where(i < EARLY, i, EARLY + turn(i) % 12)], core_peer)
 
         def hx_copy(i):
             here = hid.at[i, :, owned]
-            return remote(here, here, hx_send.at[i], hx_recv.at[i], x_peer)
+            return remote(here, here, hx_send.at[0], hx_recv.at[turn(i) % 12], x_peer)
 
         def hf_copy(i):
             there = hid.at[i, :, home]
-            return remote(there, there, hf_send.at[i], hf_recv.at[i], core_peer)
+            return remote(there, there, hf_send.at[0], hf_recv.at[turn(i) % 8], core_peer)
 
         def acc_copies(group):
             if group == 2:
-                return [remote(acc.at[2], acc_in.at[2], acc_send.at[1, 0], acc_recv.at[1, 0], tp_peers[2])]
+                return [remote(acc.at[2], acc_in.at[2], acc_send.at[0], acc_recv.at[0], tp_peers[2])]
             return [remote(acc.at[group, :, :, rows_of[way]], acc_in.at[way, :, :, rows_of[group // 2]],
-                           acc_send.at[group - 1, way], acc_recv.at[group - 1, way], tp_peers[way]) for way in range(2)]
+                           acc_send.at[0], acc_recv.at[0], tp_peers[way]) for way in range(2)]
 
         def tail_copy(kind, k):
             peer, slot = dp_peer(k)
             dst = rows.at[kind, :, pl.ds(pl.multiple_of(dp * depth, depth), depth)]
-            return remote(tail.at[kind, slot], dst, tail_send.at[kind, k - 1], tail_recv.at[kind, k - 1], {"tp": tp, "dp": peer})
+            return remote(tail.at[kind, slot], dst, tail_send.at[0], tail_recv.at[0], {"tp": tp, "dp": peer})
 
         barrier = pltpu.get_barrier_semaphore()
         for k in range(1, 4):
@@ -156,9 +162,13 @@
             near[i, x] = near[i, x] + part[i, home]
             far_copy(i).start()
 
-        for micro in range(2):
-            for kind in range(2):
-                first_copy(micro, kind, 1).wait_recv()
+        def took(ref, recv):
+            remote(ref, ref, recv, recv, core_peer).wait_recv()
+
+        def sent(ref, send):
+            remote(ref, ref, send, send, core_peer).wait_send()
+
+        took(cols.at[0, :, 0], first_recv.at[0])
         for kind in range(2):
             for copy in lead_copies(0, kind):
                 copy.start()
@@ -176,16 +186,13 @@
             return carry
 
         lax.fori_loop(0, EARLY, open_here, 0)
+        took(cols.at[0, :, 0], first_recv.at[1])
         for kind in range(2):
-            for k in (2, 3):
-                first_copy(0, kind, k).wait_recv()
             for copy in lead_copies(1, kind):
                 copy.start()
         half_sum(EARLY - 1, here_copy(EARLY - 1))
 
-        for kind in range(2):
-            for k in (2, 3):
-                first_copy(1, kind, k).wait_recv()
+        took(cols.at[0, :, 0], first_recv.at[2])
 
         def open_there(i, carry):
             half_products(i, ox)
@@ -205,9 +212,7 @@
             for other in (1, 2, 3):
                 @pl.when(i == other * chunks)
                 def _(other=other):
-                    for kind in range(2):
-                        for copy in spread_copies(other, kind) if other > 1 else lead_copies(0, kind) + lead_copies(1, kind):
-                            copy.wait_recv()
+                    took(cols.at[other], lead_recv.at[0] if other == 1 else spread_recv.at[other - 2])
 
             x_rows = cols[group, 0].reshape(SLOTS * 16, depth)
             dy_rows = cols[group, 1].reshape(SLOTS * 16, depth)
@@ -311,9 +316,7 @@
         for kind in range(2):
             (add_y, add_dx)[kind](0, last, last)
             if kind == 0:
-                for group in (1, 2, 3):
-                    for copy in acc_copies(group):
-                        copy.wait_recv()
+                took(acc_in, acc_recv.at[0])
             value = acc[0, kind] + acc_in[0, kind] + acc_in[1, kind] + acc_in[2, kind]
             tail[kind] = (cols[0, kind].astype(F32) + value).astype(BF16)
             for k in (2, 3, 1):
@@ -321,34 +324,16 @@
         for kind in range(2):
             rows[kind, :, own] = tail[kind, home]
 
-        for k in (1, 2, 3):
-            for kind in range(2):
-                spread = spread_copies(k, kind) if k > 1 else lead_copies(0, kind) + lead_copies(1, kind)
-                for copy in [first_copy(0, kind, k), first_copy(1, kind, k)] + spread:
-                    copy.wait_send()
-            for copy in acc_copies(k):
-                copy.wait_send()
-
-        def drain(i, carry):
-            @pl.when(i < EARLY)
-            def _():
-                here_copy(i).wait_send()
-                there_copy(i).wait_send()
-
-            @pl.when(i >= EARLY)
-            def _():
-                near_copy(i).wait_send()
-
-            far_copy(i).wait_send()
-            hc_copy(i).wait_send()
-            hx_copy(i).wait_send()
-            hf_copy(i).wait_send()
-            return carry
-
-        lax.fori_loop(0, total, drain, 0)
-        for kind in range(2):
-            for k in (1, 2, 3):
-                tail_copy(kind, k).wait()
+        sent(cols.at[0, :, pl.ds(0, 3)], first_send.at[0])
+        sent(cols.at[0], lead_send.at[0])
+        sent(cols.at[pl.ds(0, 2)], spread_send.at[0])
+        sent(acc_in, acc_send.at[0])
+        sent(near, near_send.at[0])
+        sent(far, far_send.at[0])
+        for send in (hc_send, hx_send, hf_send):
+            sent(hid.at[:, :, 0], send.at[0])
+        took(tail.at[:, pl.ds(0, 3)], tail_recv.at[0])
+        sent(tail.at[:, pl.ds(0, 3)], tail_send.at[0])
 
     return kernel, total
 
@@ -465,17 +450,17 @@
                 pltpu.VMEM((GROUPS - 1, 2, SLOTS, 16, depth), F32),
                 pltpu.VMEM((2, SLOTS, 16, depth), BF16),
                 dma((chunks, 3)),
-                dma((2, 2, 3)), dma((2, 2, 3)),
-                dma((3, 2, 2)), dma((3, 2, 2)),
-                dma((total,)), dma((total,)),
-                dma((total,)), dma((total,)),
-                dma((total,)), dma((total,)),
-                dma((total,)), dma((total,)),
-                dma((total,)), dma((total,)),
-                dma((3, 2)), dma((3, 2)),
-                dma((2, 3)), dma((2, 3)),
-                dma((2,)), dma((EARLY,)), dma((EARLY,)),
-                dma((2, 2, 2, 2)), dma((2, 2, 2, 2)),
+                dma((1,)), dma((3,)),
+                dma((1,)), dma((2,)),
+                dma((1,)), dma((8,)),
+                dma((1,)), dma((10,)),
+                dma((1,)), dma((EARLY + 12,)),
+                dma((1,)), dma((12,)),
+                dma((1,)), dma((8,)),
+                dma((1,)), dma((1,)),
+                dma((1,)), dma((1,)),
+                dma((2,)), dma((EARLY,)),
+                dma((1,)), dma((1,)),
             ],
             compiler_params=pltpu.CompilerParams(collective_id=0, has_side_effects=True, vmem_limit_bytes=53 * 2**20),
         )(x_loc.reshape(micro * local_rows, model), dy_loc.reshape(micro * local_rows, model), w_gate_loc, w_up_loc, w_down_loc)

time: 128 us -> 126 us (0.984)
  Pallas kernels: 128 us -> 125 us
    pallas_call x1, Pallas kernels: 113 us -> 110 us  [local_step(): pl.pallas_call(kernel, out_shape=[pltpu.VMEM((2, micro * local_rows, mode...]
where the time goes in v10:
time: 126 us; the launch traced here: 125 us
  Pallas kernels  125 us (99%)
    pallas_call x1, Pallas kernels, local_step(): pl.pallas_call(kernel, out_shape=[pltpu.VMEM((2, micro * local_rows, mode...  110 us
    pallas_call x1, Pallas kernels, finish(): pl.pallas_call(kernel, out_shape=[row_shape, row_shape, jax.ShapeDtypeStr...  14.7 us

profile of v10, /device:TPU:0, one launch (start us, length us, event | category | flops | bytes accessed | tf_op | source)
XLA Modules:
  0.0 125.4 jit_solution(14189915275094462824)
XLA Ops:
  0.6 110.1 %shard_map.92 = (bf16[2,16,4096]{2,1,0:T(8,128)(2,1)S(1)}, bf16[28,3,4,16,512]{4,3,2,1,0:T(8,128)(2,1)S(1)}, bf16[4,2,4,16,1024]{4,3,2,1,0:T(8,128)(2,1)S(1)}, bf16[1024,256]{1,0:T(8,128)(2,1)S(1)}) custom-call(bf16[16,4096]{1,0:T(8,128)(2,1)} %bitcast.4, bf16[16,4096]{1,0:T(8,128)(2,1)} %bitcast.5, bf16[1024,3584]{1,0:T(8,128)(2,1)} %wg_hbm.1, ...), custom_call_target="tpu_custom_call" | custom-call | tf_op jit(solution)/shard_map/pallas_call | solution.py:430
  110.7 14.7 %shard_map.93 = (bf16[16,4096]{1,0:T(8,128)(2,1)}, bf16[16,4096]{1,0:T(8,128)(2,1)}, f32[1024,3584]{1,0:T(8,128)}, f32[1024,3584]{1,0:T(8,128)}, f32[3584,1024]{1,0:T(8,128)}) custom-call(bf16[2,16,4096]{2,1,0:T(8,128)(2,1)S(1)} %get-tuple-element.14.rows_ref, bf16[28,3,4,16,512]{4,3,2,1,0:T(8,128)(2,1)S(1)} %get-tuple-element.15.hid_ref, ...), custom_call_target="tpu_custom_call" | custom-call | flops 5637144576 | bytes 44040192 | tf_op jit(solution)/shard_map/pallas_call | solution.py:400

commit v11 on v10

--- a/solution.py
+++ b/solution.py
@@ -63,9 +63,13 @@
 
         def weight_copies(c):
             span = pl.ds(pl.multiple_of(c * width, width), width)
-            return (pltpu.make_async_copy(wg_hbm.at[:, span], wg.at[c], w_sem.at[c, 0]),
-                    pltpu.make_async_copy(wu_hbm.at[:, span], wu.at[c], w_sem.at[c, 1]),
-                    pltpu.make_async_copy(wd_hbm.at[span], wd.at[c], w_sem.at[c, 2]))
+            return (pltpu.make_async_copy(wg_hbm.at[:, span], wg.at[c], w_sem.at[c]),
+                    pltpu.make_async_copy(wu_hbm.at[:, span], wu.at[c], w_sem.at[c]),
+                    pltpu.make_async_copy(wd_hbm.at[span], wd.at[c], w_sem.at[c]))
+
+        def weights_in(c):
+            size = part.at[pl.ds(0, 8)]
+            pltpu.make_async_copy(size, size, w_sem.at[c]).wait()
 
         def remote(src, dst, send, recv, device):
             return pltpu.make_async_remote_copy(src_ref=src, dst_ref=dst, send_sem=send, recv_sem=recv,
@@ -174,8 +178,7 @@
                 copy.start()
 
         def open_here(i, carry):
-            for copy in weight_copies(i):
-                copy.wait()
+            weights_in(i)
             half_products(i, x)
             here_copy(i).start()
 
@@ -206,8 +209,7 @@
 
             @pl.when(jnp.logical_and(group == 1, c >= EARLY))
             def _():
-                for copy in weight_copies(c):
-                    copy.wait()
+                weights_in(c)
 
             for other in (1, 2, 3):
                 @pl.when(i == other * chunks)
@@ -259,6 +261,11 @@
                         copy.start()
 
         def step(s, carry):
+            @pl.when(jnp.logical_and(s > EARLY, s < total + 1))
+            def _():
+                i = chunk_at(s - 1)
+                half_sum(i, near_copy(i))
+
             @pl.when(s < total)
             def _():
                 products(chunk_at(s))
@@ -269,11 +276,6 @@
                     for kind in range(2):
                         for copy in spread_copies(other, kind):
                             copy.start()
-
-            @pl.when(jnp.logical_and(s > EARLY, s < total + 1))
-            def _():
-                i = chunk_at(s - 1)
-                half_sum(i, near_copy(i))
 
             @pl.when(jnp.logical_and(s >= FINAL_LAG, s < total + FINAL_LAG))
             def _():
@@ -449,7 +451,7 @@
                 pltpu.VMEM((GROUPS, 2, SLOTS, 16, depth), F32),
                 pltpu.VMEM((GROUPS - 1, 2, SLOTS, 16, depth), F32),
                 pltpu.VMEM((2, SLOTS, 16, depth), BF16),
-                dma((chunks, 3)),
+                dma((chunks,)),
                 dma((1,)), dma((3,)),
                 dma((1,)), dma((2,)),
                 dma((1,)), dma((8,)),

time: 126 us -> 125 us (level)
  no operation moved by 1% of the time
where the time goes in v11:
time: 125 us
  Pallas kernels  125 us (100%)
    pallas_call x1, Pallas kernels, local_step(): pl.pallas_call(kernel, out_shape=[pltpu.VMEM((2, micro * local_rows, mode...  110 us
    pallas_call x1, Pallas kernels, finish(): pl.pallas_call(kernel, out_shape=[row_shape, row_shape, jax.ShapeDtypeStr...  14.7 us

profile of v11, /device:TPU:0, one launch (start us, length us, event | category | flops | bytes accessed | tf_op | source)
XLA Modules:
  0.0 125.3 jit_solution(13782863295607099050)
XLA Ops:
  0.6 109.9 %shard_map.92 = (bf16[2,16,4096]{2,1,0:T(8,128)(2,1)S(1)}, bf16[28,3,4,16,512]{4,3,2,1,0:T(8,128)(2,1)S(1)}, bf16[4,2,4,16,1024]{4,3,2,1,0:T(8,128)(2,1)S(1)}, bf16[1024,256]{1,0:T(8,128)(2,1)S(1)}) custom-call(bf16[16,4096]{1,0:T(8,128)(2,1)} %bitcast.4, bf16[16,4096]{1,0:T(8,128)(2,1)} %bitcast.5, bf16[1024,3584]{1,0:T(8,128)(2,1)} %wg_hbm.1, ...), custom_call_target="tpu_custom_call" | custom-call | tf_op jit(solution)/shard_map/pallas_call | solution.py:432
  110.6 14.7 %shard_map.93 = (bf16[16,4096]{1,0:T(8,128)(2,1)}, bf16[16,4096]{1,0:T(8,128)(2,1)}, f32[1024,3584]{1,0:T(8,128)}, f32[1024,3584]{1,0:T(8,128)}, f32[3584,1024]{1,0:T(8,128)}) custom-call(bf16[2,16,4096]{2,1,0:T(8,128)(2,1)S(1)} %get-tuple-element.14.rows_ref, bf16[28,3,4,16,512]{4,3,2,1,0:T(8,128)(2,1)S(1)} %get-tuple-element.15.hid_ref, ...), custom_call_target="tpu_custom_call" | custom-call | flops 5637144576 | bytes 44040192 | tf_op jit(solution)/shard_map/pallas_call | solution.py:402

commit v12 on v11

--- a/solution.py
+++ b/solution.py
@@ -13,7 +13,7 @@
 FINAL_LAG = 4
 FORWARD_LAG = 10
 BACK_LAG = 11
-EARLY = 4
+EARLY = 3
 
 
 def dot(lhs, rhs):

time: 125 us -> 126 us (level)
  no operation moved by 1% of the time
where the time goes in v12:
time: 126 us
  Pallas kernels  125 us (99%)
    pallas_call x1, Pallas kernels, local_step(): pl.pallas_call(kernel, out_shape=[pltpu.VMEM((2, micro * local_rows, mode...  110 us
    pallas_call x1, Pallas kernels, finish(): pl.pallas_call(kernel, out_shape=[row_shape, row_shape, jax.ShapeDtypeStr...  14.7 us

profile of v12, /device:TPU:0, one launch (start us, length us, event | category | flops | bytes accessed | tf_op | source)
XLA Modules:
  0.0 125.8 jit_solution(2341150573957418852)
XLA Ops:
  0.6 110.5 %shard_map.92 = (bf16[2,16,4096]{2,1,0:T(8,128)(2,1)S(1)}, bf16[28,3,4,16,512]{4,3,2,1,0:T(8,128)(2,1)S(1)}, bf16[4,2,4,16,1024]{4,3,2,1,0:T(8,128)(2,1)S(1)}, bf16[1024,256]{1,0:T(8,128)(2,1)S(1)}) custom-call(bf16[16,4096]{1,0:T(8,128)(2,1)} %bitcast.4, bf16[16,4096]{1,0:T(8,128)(2,1)} %bitcast.5, bf16[1024,3584]{1,0:T(8,128)(2,1)} %wg_hbm.1, ...), custom_call_target="tpu_custom_call" | custom-call | tf_op jit(solution)/shard_map/pallas_call | solution.py:432
  111.1 14.7 %shard_map.93 = (bf16[16,4096]{1,0:T(8,128)(2,1)}, bf16[16,4096]{1,0:T(8,128)(2,1)}, f32[1024,3584]{1,0:T(8,128)}, f32[1024,3584]{1,0:T(8,128)}, f32[3584,1024]{1,0:T(8,128)}) custom-call(bf16[2,16,4096]{2,1,0:T(8,128)(2,1)S(1)} %get-tuple-element.14.rows_ref, bf16[28,3,4,16,512]{4,3,2,1,0:T(8,128)(2,1)S(1)} %get-tuple-element.15.hid_ref, ...), custom_call_target="tpu_custom_call" | custom-call | flops 5637144576 | bytes 44040192 | tf_op jit(solution)/shard_map/pallas_call | solution.py:402

commit v13 on v12

--- a/solution.py
+++ b/solution.py
@@ -11,9 +11,9 @@
 GROUPS = 4
 SLOTS = 4
 FINAL_LAG = 4
-FORWARD_LAG = 10
-BACK_LAG = 11
-EARLY = 3
+FORWARD_LAG = 11
+BACK_LAG = 12
+EARLY = 5
 
 
 def dot(lhs, rhs):
@@ -285,7 +285,7 @@
             def _():
                 hx_copy(s - FINAL_LAG + chunks - EARLY).start()
 
-            @pl.when(s == total)
+            @pl.when(s == total - chunks + EARLY + FINAL_LAG - 1)
             def _():
                 for c in range(EARLY):
                     hx_copy(c).start()
@@ -310,6 +310,8 @@
 
             return carry
 
+        for c in range(EARLY - FINAL_LAG):
+            activations(c)
         lax.fori_loop(EARLY, total + BACK_LAG - 1, step, 0)
 
         last = chunks - 1

time: 126 us -> 126 us (level)
  no operation moved by 1% of the time
where the time goes in v13:
time: 126 us
  Pallas kernels  125 us (99%)
    pallas_call x1, Pallas kernels, local_step(): pl.pallas_call(kernel, out_shape=[pltpu.VMEM((2, micro * local_rows, mode...  110 us
    pallas_call x1, Pallas kernels, finish(): pl.pallas_call(kernel, out_shape=[row_shape, row_shape, jax.ShapeDtypeStr...  14.7 us

profile of v13, /device:TPU:0, one launch (start us, length us, event | category | flops | bytes accessed | tf_op | source)
XLA Modules:
  0.0 125.8 jit_solution(7356108716426288728)
XLA Ops:
  0.6 110.4 %shard_map.92 = (bf16[2,16,4096]{2,1,0:T(8,128)(2,1)S(1)}, bf16[28,3,4,16,512]{4,3,2,1,0:T(8,128)(2,1)S(1)}, bf16[4,2,4,16,1024]{4,3,2,1,0:T(8,128)(2,1)S(1)}, bf16[1024,256]{1,0:T(8,128)(2,1)S(1)}) custom-call(bf16[16,4096]{1,0:T(8,128)(2,1)} %bitcast.4, bf16[16,4096]{1,0:T(8,128)(2,1)} %bitcast.5, bf16[1024,3584]{1,0:T(8,128)(2,1)} %wg_hbm.1, ...), custom_call_target="tpu_custom_call" | custom-call | tf_op jit(solution)/shard_map/pallas_call | solution.py:434
  111.1 14.7 %shard_map.93 = (bf16[16,4096]{1,0:T(8,128)(2,1)}, bf16[16,4096]{1,0:T(8,128)(2,1)}, f32[1024,3584]{1,0:T(8,128)}, f32[1024,3584]{1,0:T(8,128)}, f32[3584,1024]{1,0:T(8,128)}) custom-call(bf16[2,16,4096]{2,1,0:T(8,128)(2,1)S(1)} %get-tuple-element.14.rows_ref, bf16[28,3,4,16,512]{4,3,2,1,0:T(8,128)(2,1)S(1)} %get-tuple-element.15.hid_ref, ...), custom_call_target="tpu_custom_call" | custom-call | flops 5637144576 | bytes 44040192 | tf_op jit(solution)/shard_map/pallas_call | solution.py:404

commit v14 on v11

--- a/solution.py
+++ b/solution.py
@@ -106,19 +106,19 @@
             return open_copy(i, ox, near_recv.at[i % 8])
 
         def far_copy(i):
-            return remote(near.at[i, x], far.at[i], far_send.at[0], far_recv.at[place(i) % 10], x_peer)
+            return remote(near.at[i, x], far.at[i], far_send.at[0], far_recv.at[place(i) % 8], x_peer)
 
         def hc_copy(i):
             here = hid.at[i, :, owned]
-            return remote(here, here, hc_send.at[0], hc_recv.at[jnp.where(i < EARLY, i, EARLY + turn(i) % 12)], core_peer)
+            return remote(here, here, hc_send.at[0], hc_recv.at[jnp.where(i < EARLY, i, EARLY + turn(i) % 10)], core_peer)
 
         def hx_copy(i):
             here = hid.at[i, :, owned]
-            return remote(here, here, hx_send.at[0], hx_recv.at[turn(i) % 12], x_peer)
+            return remote(here, here, hx_send.at[0], hx_recv.at[turn(i) % 10], x_peer)
 
         def hf_copy(i):
             there = hid.at[i, :, home]
-            return remote(there, there, hf_send.at[0], hf_recv.at[turn(i) % 8], core_peer)
+            return remote(there, there, hf_send.at[0], hf_recv.at[turn(i) % 6], core_peer)
 
         def acc_copies(group):
             if group == 2:
@@ -455,10 +455,10 @@
                 dma((1,)), dma((3,)),
                 dma((1,)), dma((2,)),
                 dma((1,)), dma((8,)),
+                dma((1,)), dma((8,)),
+                dma((1,)), dma((EARLY + 10,)),
                 dma((1,)), dma((10,)),
-                dma((1,)), dma((EARLY + 12,)),
-                dma((1,)), dma((12,)),
-                dma((1,)), dma((8,)),
+                dma((1,)), dma((6,)),
                 dma((1,)), dma((1,)),
                 dma((1,)), dma((1,)),
                 dma((2,)), dma((EARLY,)),

time: 125 us -> 125 us (level)
  no operation moved by 1% of the time
where the time goes in v14:
time: 125 us
  Pallas kernels  125 us (100%)
    pallas_call x1, Pallas kernels, local_step(): pl.pallas_call(kernel, out_shape=[pltpu.VMEM((2, micro * local_rows, mode...  110 us
    pallas_call x1, Pallas kernels, finish(): pl.pallas_call(kernel, out_shape=[row_shape, row_shape, jax.ShapeDtypeStr...  14.7 us

profile of v14, /device:TPU:0, one launch (start us, length us, event | category | flops | bytes accessed | tf_op | source)
XLA Modules:
  0.0 125.2 jit_solution(4380130799321821019)
XLA Ops:
  0.6 109.9 %shard_map.92 = (bf16[2,16,4096]{2,1,0:T(8,128)(2,1)S(1)}, bf16[28,3,4,16,512]{4,3,2,1,0:T(8,128)(2,1)S(1)}, bf16[4,2,4,16,1024]{4,3,2,1,0:T(8,128)(2,1)S(1)}, bf16[1024,256]{1,0:T(8,128)(2,1)S(1)}) custom-call(bf16[16,4096]{1,0:T(8,128)(2,1)} %bitcast.4, bf16[16,4096]{1,0:T(8,128)(2,1)} %bitcast.5, bf16[1024,3584]{1,0:T(8,128)(2,1)} %wg_hbm.1, ...), custom_call_target="tpu_custom_call" | custom-call | tf_op jit(solution)/shard_map/pallas_call | solution.py:432
  110.5 14.7 %shard_map.93 = (bf16[16,4096]{1,0:T(8,128)(2,1)}, bf16[16,4096]{1,0:T(8,128)(2,1)}, f32[1024,3584]{1,0:T(8,128)}, f32[1024,3584]{1,0:T(8,128)}, f32[3584,1024]{1,0:T(8,128)}) custom-call(bf16[2,16,4096]{2,1,0:T(8,128)(2,1)S(1)} %get-tuple-element.14.rows_ref, bf16[28,3,4,16,512]{4,3,2,1,0:T(8,128)(2,1)S(1)} %get-tuple-element.15.hid_ref, ...), custom_call_target="tpu_custom_call" | custom-call | flops 5637144576 | bytes 44040192 | tf_op jit(solution)/shard_map/pallas_call | solution.py:402
